TPU v7x, 1024 devices: a whole 4x4x32 slice. The times are simulated.
1024 devices in a mesh: gx: 128 (over z, y), gy: 8 (over x, core).
Axes of the slice: x: 4, y: 4, z: 32, core: 2. Of those that a mesh axis runs over, the one named last changes fastest.
Arguments:
- residual_block: float32 [8, 512, 64, 256], P(None, 'gx', 'gy'), may hold values from -70 to 70
- diagonal: float32 [512, 64, 256], P('gx', 'gy'), may hold values from 0.5 to 4
Outputs:
- correction: float32 [8, 512, 64, 256], P(None, 'gx', 'gy')
- new_residual: float32 [8, 512, 64, 256], P(None, 'gx', 'gy')
- estimate: float32 [8], replicated
All inputs are finite; a program needn't handle non-finite values.
Results may differ from a plain program's by a relative error of at most 0.008.
Values sent between devices are 32-bit elements; how exact they have to be, the bound alone decides.
No kernel may reach another device: no remote copies, remote signals or barrier semaphores. Data moves between devices by JAX's collectives and lax.ppermute only.
A program may use at most 32 MiB of HBM per device.

v0:
```python
import jax
import jax.numpy as jnp
import numpy as np
from jax import lax
from jax.sharding import Mesh
from jax.sharding import PartitionSpec as P

NRHS = 8
GX = ("gx_0", "gx_1")


WEIGHT_X = 0.4
WEIGHT_Y = 0.2
WEIGHT_Z = 0.1
CENTRE = 2.2
SCALE_POWER = 3.0
SHIFTS = (6.0, 1.5, 4.5, 3.0)
EPSILON = 1e-06


def padded_2(block, sides, width):
    for axis, dim in sides:
        count = lax.axis_size(axis)
        forward = [(i, i + 1) for i in range(count - 1)]
        backward = [(target, source) for source, target in forward]
        low = lax.ppermute(
            lax.slice_in_dim(block, block.shape[dim] - width, None, axis=dim), axis, forward
        )
        high = lax.ppermute(lax.slice_in_dim(block, 0, width, axis=dim), axis, backward)
        block = jnp.concatenate([low, block, high], axis=dim)
    return block


def sent_to_all(x, axis):
    count = lax.axis_size(axis)
    return lax.all_to_all(jnp.broadcast_to(x[None], (count, *x.shape)), axis, 0, 0, tiled=True)


def over_copies(x, axis):
    return sent_to_all(x, axis).sum(axis=0)


def one_axis_at_a_time(x, axes):
    for axis in axes:
        x = lax.psum(x, axis)
    return x


def apply_padded(padded, diag_inner, shift_now):
    along_z = jnp.pad(padded, ((0, 0), (0, 0), (0, 0), (1, 1)))
    sum_z = padded + WEIGHT_Z * (along_z[..., :-2] + along_z[..., 2:])
    sum_y = sum_z[:, :, 1:-1] + WEIGHT_Y * (sum_z[:, :, :-2] + sum_z[:, :, 2:])
    sum_x = sum_y[:, 1:-1] + WEIGHT_X * (sum_y[:, :-2] + sum_y[:, 2:])
    centre_cells = padded[:, 1:-1, 1:-1]
    return ((CENTRE + 1.0 + diag_inner - shift_now) * centre_cells - sum_x) / SCALE_POWER


def newton_table():
    blocks = len(SHIFTS)
    identity = np.eye(NRHS, dtype=np.float32)
    matrix = np.zeros(((blocks + 1) * NRHS, blocks * NRHS), np.float32)
    for block_index in range(blocks):
        low = block_index * NRHS
        matrix[low : low + NRHS, low : low + NRHS] = SHIFTS[block_index] * identity
        matrix[low + NRHS : low + 2 * NRHS, low : low + NRHS] = SCALE_POWER * identity
    return matrix


def solve_small(gram_full):
    highest = lax.Precision.HIGHEST
    newton = jnp.asarray(newton_table(), gram_full.dtype)
    image = jnp.dot(newton.T, jnp.dot(gram_full, newton, precision=highest), precision=highest)
    right_side = jnp.dot(newton.T, gram_full[:, :NRHS], precision=highest)
    scales = lax.rsqrt(jnp.diagonal(image) + EPSILON)
    scaled = image * scales[:, None] * scales[None, :]
    factor = jnp.linalg.cholesky(scaled)
    coeffs = scales[:, None] * jax.scipy.linalg.cho_solve(
        (factor, True), scales[:, None] * right_side
    )
    initial_sq = jnp.diagonal(gram_full)[:NRHS]
    estimate = (initial_sq - jnp.sum(right_side * coeffs, axis=0)) / initial_sq
    return (coeffs, jnp.dot(newton, coeffs, precision=highest), estimate)


def body(residual_block, diagonal):
    highest = lax.Precision.HIGHEST
    width_rhs, cells_x, cells_y, cells_z = residual_block.shape
    total_x = cells_x * lax.axis_size(GX)
    total_y = cells_y * lax.axis_size("gy")
    powers = [residual_block]
    depth = len(SHIFTS)
    outgoing = jnp.concatenate([residual_block, diagonal[None]], 0)
    extended = padded_2(outgoing, ((GX, 1), ("gy", 2)), depth)
    field_now = extended[:width_rhs]
    diag_wide = extended[width_rhs]
    coord_x = (
        lax.axis_index(GX) * cells_x - depth + jnp.arange(cells_x + 2 * depth, dtype=jnp.int32)
    )
    coord_y = (
        lax.axis_index("gy") * cells_y - depth + jnp.arange(cells_y + 2 * depth, dtype=jnp.int32)
    )
    inside_x = (coord_x >= 0) & (coord_x < total_x)
    inside_y = (coord_y >= 0) & (coord_y < total_y)
    for step_index, shift_now in enumerate(SHIFTS):
        margin = depth - 1 - step_index
        lower = depth - margin
        span_x = cells_x + 2 * margin
        span_y = cells_y + 2 * margin
        diag_now = diag_wide[lower : lower + span_x, lower : lower + span_y]
        field_now = apply_padded(field_now, diag_now, shift_now)
        inside = (
            inside_x[lower : lower + span_x][:, None] & inside_y[lower : lower + span_y][None, :]
        )
        field_now = jnp.where(inside[None, :, :, None], field_now, 0.0)
        powers.append(field_now[:, margin : margin + cells_x, margin : margin + cells_y])
    basis = jnp.concatenate(powers, 0).reshape(len(powers) * width_rhs, -1)
    local_gram = lax.dot_general(
        basis,
        basis,
        (((1,), (1,)), ((), ())),
        precision=highest,
        preferred_element_type=jnp.float32,
    )
    gram_part = over_copies(local_gram, "gy")
    gram_full = one_axis_at_a_time(gram_part, GX)
    coeffs, combined, estimate = solve_small(gram_full)
    kept = len(SHIFTS) * width_rhs
    correction = lax.dot_general(
        coeffs,
        basis[:kept],
        (((0,), (0,)), ((), ())),
        precision=highest,
        preferred_element_type=jnp.float32,
    )
    removed = lax.dot_general(
        combined,
        basis,
        (((0,), (0,)), ((), ())),
        precision=highest,
        preferred_element_type=jnp.float32,
    )
    new_residual = residual_block - removed.reshape(residual_block.shape)
    return (correction.reshape(residual_block.shape), new_residual, estimate)


def solution(mesh):
    split = Mesh(mesh.devices.reshape(32, 4, mesh.shape["gy"]), ("gx_0", "gx_1", "gy"))
    placed = (P(None, GX, "gy", None), P(GX, "gy", None))
    return jax.shard_map(
        body,
        mesh=split,
        in_specs=placed,
        out_specs=(P(None, GX, "gy", None), P(None, GX, "gy", None), P()),
        check_vma=False,
    )
```

profile of v0, /device:TPU:2, one launch (start us, length us, event | category | flops | bytes accessed | tf_op | source)
XLA Modules:
  0.0 205.0 jit_solution(18228487890761249168)
XLA Ops:
  0.6 1.1 constant_dynamic-update-slice_fusion.4
  1.8 0.8 broadcast_in_dim.61
  2.7 1.3 collective-permute-start.1
  4.0 4.6 %collective-permute-start = (f32[9,4,8,256]{3,0,2,1:T(8,128)S(1)}, f32[9,4,8,256]{3,0,2,1:T(8,128)S(1)}, u32[]{:S(2)}, u32[]{:S(2)}) collective-permute-start(f32[9,4,8,256]{3,0,2,1:T(8,128)S(1)} %dynamic-update-slice.9), channel_id=1, source_target_pairs={{0,8},{8,16},{16,24},{24,32},{32,40},{40,48},{48,56},{56,64},{64,7... | collective-permute-start | bytes 884744 | tf_op jit(solution)/shard_map/ppermute | solution.py:26
  9.4 8.9 %collective-permute-done.1 = f32[9,4,8,256]{3,0,2,1:T(8,128)S(1)} collective-permute-done((f32[9,4,8,256]{3,0,2,1:T(8,128)S(1)}, f32[9,4,8,256]{3,0,2,1:T(8,128)S(1)}, u32[]{:S(2)}, u32[]{:S(2)}) %collective-permute-start.1) | collective-permute-done | bytes 294944 | tf_op jit(solution)/shard_map/ppermute | solution.py:29
  18.3 1.2 collective-permute-done
  19.7 0.3 copy.41
  20.0 1.9 collective-permute-start.3
  21.9 0.3 copy.40
  22.2 2.4 %collective-permute-start.2 = (f32[9,12,4,256]{3,2,1,0:T(4,128)S(1)}, f32[9,12,4,256]{3,2,1,0:T(4,128)S(1)}, u32[]{:S(2)}, u32[]{:S(2)}) collective-permute-start(f32[9,12,4,256]{3,2,1,0:T(4,128)S(1)} %copy.40), channel_id=1, source_target_pairs={{0,1},{1,2},{2,3},{3,4},{4,5},{5,6},{6,7},{8,9},{9,10},{10,11},{11... | collective-permute-start | bytes 1327112 | tf_op jit(solution)/shard_map/ppermute | solution.py:26
  24.8 2.9 %collective-permute-done.3 = f32[9,12,4,256]{3,2,1,0:T(4,128)S(1)} collective-permute-done((f32[9,12,4,256]{3,2,1,0:T(4,128)S(1)}, f32[9,12,4,256]{3,2,1,0:T(4,128)S(1)}, u32[]{:S(2)}, u32[]{:S(2)}) %collective-permute-start.3) | collective-permute-done | bytes 442400 | tf_op jit(solution)/shard_map/ppermute | solution.py:29
  27.7 0.3 copy.43
  28.0 11.2 %collective-permute-done.2 = f32[9,12,4,256]{3,2,1,0:T(4,128)S(1)} collective-permute-done((f32[9,12,4,256]{3,2,1,0:T(4,128)S(1)}, f32[9,12,4,256]{3,2,1,0:T(4,128)S(1)}, u32[]{:S(2)}, u32[]{:S(2)}) %collective-permute-start.2) | collective-permute-done | bytes 442400 | tf_op jit(solution)/shard_map/ppermute | solution.py:26
  39.2 0.3 copy.42
  39.4 0.2 pad_maximum_fusion.6
  39.8 0.2 pad_maximum_fusion
  40.0 0.9 fusion.2
  41.0 0.8 fusion.17
  41.8 0.7 fusion.12
  42.6 0.3 fusion.29
  42.9 0.5 fusion.24
  43.5 0.2 fusion.39
  43.6 0.3 fusion.34
  44.2 1.2 convolution_bitcast_fusion
  45.3 0.8 reshape.172
  46.1 3.3 %all-to-all-start = ((f32[8,1,1600]{2,1,0:T(1,128)}), f32[8,1,1600]{2,1,0:T(1,128)S(1)}, u32[]{:S(2)}, u32[]{:S(2)}) async-start(f32[8,1,1600]{2,1,0:T(1,128)} %reshape.172), calls=%async_computation | async-start | bytes 106496 | tf_op jit(solution)/shard_map/all_to_all | solution.py:36
  49.5 1.6 copy.59
  51.1 0.4 copy.61
  51.6 2.0 all-to-all-done
  53.5 0.5 broadcast.256
  54.0 0.8 reduce.6
  55.0 121.0 %psum.14 = f32[40,40]{1,0:T(8,128)S(1)} all-reduce(f32[40,40]{1,0:T(8,128)S(1)} %reduce_sum.18), channel_id=1, replica_groups=mesh['gx_0'=32,'gx_1'=4,'gy'=8] {'gx_0'}, use_global_device_ids=true, to_apply=%region_1.2 | all-reduce | flops 1600 | bytes 12800 | tf_op jit(solution)/shard_map/psum | solution.py:45
  175.9 14.6 %psum.15 = f32[40,40]{1,0:T(8,128)S(1)} all-reduce(f32[40,40]{1,0:T(8,128)S(1)} %psum.14), channel_id=1, replica_groups=mesh['gx_0'=32,'gx_1'=4,'gy'=8] {'gx_1'}, use_global_device_ids=true, to_apply=%region_2.3 | all-reduce | flops 1600 | bytes 12800 | tf_op jit(solution)/shard_map/psum | solution.py:45
  190.5 0.2 fusion.48
  190.7 0.2 fusion.58
  191.2 0.7 gather_fusion
  192.0 2.9 %cholesky.16 = f32[32,32]{1,0:T(8,128)S(1)} custom-call(f32[32,32]{1,0:T(8,128)S(1)} %add_multiply_fusion), custom_call_target="Cholesky" | custom-call | tf_op jit(solution)/shard_map/jit(cholesky)/cholesky | solution.py:76
  194.9 0.6 compare_reduce_fusion
  195.6 0.7 fusion.50
  196.2 2.4 %custom-call.10 = f32[1,32,32]{1,2,0:T(8,128)S(1)} custom-call(f32[1,32,32]{2,1,0:T(8,128)S(1)} %fusion.50), custom_call_target="InvertDiagBlocksLowerTriangular" | custom-call | tf_op jit(solution)/shard_map/jit(_cho_solve)/triangular_solve | solution.py:77
  198.7 0.2 fusion.52
  198.8 0.3 multiply_reduce_fusion
  199.2 1.2 fusion.18
  200.4 0.8 copy.52
  201.2 1.5 fusion.7
  202.7 0.8 copy.53
  203.5 1.0 gather_fusion.1
  204.5 0.5 subtract_divide_fusion
  (48 shorter events, 2.7 us)
Async XLA Ops:
  2.7 15.6 %collective-permute-start.1 = (f32[9,4,8,256]{3,0,2,1:T(8,128)S(1)}, f32[9,4,8,256]{3,0,2,1:T(8,128)S(1)}, u32[]{:S(2)}, u32[]{:S(2)}) collective-permute-start(f32[9,4,8,256]{3,0,2,1:T(8,128)S(1)} %dynamic-update-slice.9), channel_id=1, source_target_pairs={{8,0},{16,8},{24,16},{32,24},{40,32},{48,40},{56,48},{64,56},{72,6... | collective-permute-start | bytes 884744 | tf_op jit(solution)/shard_map/ppermute | solution.py:29
  4.0 15.4 %collective-permute-start = (f32[9,4,8,256]{3,0,2,1:T(8,128)S(1)}, f32[9,4,8,256]{3,0,2,1:T(8,128)S(1)}, u32[]{:S(2)}, u32[]{:S(2)}) collective-permute-start(f32[9,4,8,256]{3,0,2,1:T(8,128)S(1)} %dynamic-update-slice.9), channel_id=1, source_target_pairs={{0,8},{8,16},{16,24},{24,32},{32,40},{40,48},{48,56},{56,64},{64,7... | collective-permute-start | bytes 884744 | tf_op jit(solution)/shard_map/ppermute | solution.py:26
  20.0 7.7 %collective-permute-start.3 = (f32[9,12,4,256]{3,2,1,0:T(4,128)S(1)}, f32[9,12,4,256]{3,2,1,0:T(4,128)S(1)}, u32[]{:S(2)}, u32[]{:S(2)}) collective-permute-start(f32[9,12,4,256]{3,2,1,0:T(4,128)S(1)} %copy.41), channel_id=1, source_target_pairs={{1,0},{2,1},{3,2},{4,3},{5,4},{6,5},{7,6},{9,8},{10,9},{11,10},{12... | collective-permute-start | bytes 1327112 | tf_op jit(solution)/shard_map/ppermute | solution.py:29
  22.2 16.9 %collective-permute-start.2 = (f32[9,12,4,256]{3,2,1,0:T(4,128)S(1)}, f32[9,12,4,256]{3,2,1,0:T(4,128)S(1)}, u32[]{:S(2)}, u32[]{:S(2)}) collective-permute-start(f32[9,12,4,256]{3,2,1,0:T(4,128)S(1)} %copy.40), channel_id=1, source_target_pairs={{0,1},{1,2},{2,3},{3,4},{4,5},{5,6},{6,7},{8,9},{9,10},{10,11},{11... | collective-permute-start | bytes 1327112 | tf_op jit(solution)/shard_map/ppermute | solution.py:26
  46.1 7.4 %all-to-all-start = ((f32[8,1,1600]{2,1,0:T(1,128)}), f32[8,1,1600]{2,1,0:T(1,128)S(1)}, u32[]{:S(2)}, u32[]{:S(2)}) async-start(f32[8,1,1600]{2,1,0:T(1,128)} %reshape.172), calls=%async_computation | async-start | bytes 106496 | tf_op jit(solution)/shard_map/all_to_all | solution.py:36
  51.1 139.4 %copy-start.2 = (f32[40,32]{1,0:T(8,128)S(1)}, f32[40,32]{1,0:T(8,128)}, u32[]{:S(2)}) copy-start(f32[40,32]{1,0:T(8,128)} %constant.137.clone) | copy-start | bytes 15364
  51.6 147.7 %copy-start = (f32[4,8,32,256]{3,2,1,0:T(8,128)S(1)}, f32[4,8,32,256]{3,2,1,0:T(8,128)}, u32[]{:S(2)}) copy-start(f32[4,8,32,256]{3,2,1,0:T(8,128)} %copy.59) | copy-start | bytes 3145732
  191.1 10.1 %copy-start.1 = (f32[8,4,8,256]{3,2,1,0:T(8,128)S(1)}, f32[8,4,8,256]{3,2,1,0:T(8,128)}, u32[]{:S(2)}) copy-start(f32[8,4,8,256]{3,2,1,0:T(8,128)} %param.3) | copy-start | bytes 786436
where the time goes:
time: 205 us
  blocking collectives  136 us (66%)
  waiting for transfers between devices  26.1 us (13%)
  starting transfers between devices  13.5 us (7%)
  other arithmetic  13.1 us (6%)
  local copies, waits for them, and re-layouts  10.8 us (5%)
  matrix products  4.96 us (2%)
    psum x2, blocking collectives, one_axis_at_a_time(): x = lax.psum(x, axis)  136 us
    ppermute x2, waiting for transfers between devices, padded_2(): lax.ppermute(lax.slice_in_dim(block, block.shape[dim] - width, None, axis...  12.3 us
    ppermute x2, waiting for transfers between devices, padded_2(): lax.ppermute(lax.slice_in_dim(block, 0, width, axis=dim), axis, backward)  11.8 us
    ppermute x2, starting transfers between devices, padded_2(): lax.ppermute(lax.slice_in_dim(block, block.shape[dim] - width, None, axis...  6.99 us
    unnamed x17, local copies, waits for them, and re-layouts  5.73 us
  transfers between devices with their start and end apart: 5, of which 5 were waited for; matrix products, arithmetic and copies ran while one was open for 2% of the time, Pallas kernels for 0%

commit v1 on v0

v1 whole, which is shorter than its diff:
```python
import functools

import jax
import jax.numpy as jnp
import numpy as np
from jax import lax
from jax.experimental import pallas as pl
from jax.experimental.pallas import tpu as pltpu
from jax.sharding import Mesh
from jax.sharding import PartitionSpec as P

NRHS = 8
WEIGHT_X = 0.4
WEIGHT_Y = 0.2
WEIGHT_Z = 0.1
CENTRE = 2.2
SCALE_POWER = 3.0
SHIFTS = (6.0, 1.5, 4.5, 3.0)
DEPTH = len(SHIFTS)

CX, CY, CZ = 4, 8, 256
WX, WY = CX + 2 * DEPTH, CY + 2 * DEPTH
LANES = 128
HIGHEST = lax.Precision.HIGHEST

GX = ("z1", "z0", "y")
NEAR = ("z0", "y", "gy")
FAR = ("z1",)
OWN = CX * CY
PACK = OWN + CX
SIDE = WX * DEPTH
SIDE_PACK = SIDE + WX // 2


def moment_terms():
    table = {}
    for j in range(DEPTH + 1):
        for i in (j, j + 1):
            if i <= DEPTH:
                table[i, j] = np.eye(9)[2 * j + (i - j)]
    for gap in range(2, DEPTH + 1):
        for j in range(DEPTH + 1 - gap):
            i = j + gap - 1
            low = table[i, j + 1]
            table[i + 1, j] = low + (SHIFTS[j] - SHIFTS[i]) / SCALE_POWER * table[i, j]

    def block(i, j):
        return table[max(i, j), min(i, j)]

    alpha = np.zeros((9, DEPTH, DEPTH + 1))
    for i in range(DEPTH):
        for j in range(DEPTH):
            alpha[:, i, j] = (
                SHIFTS[i] * SHIFTS[j] * block(i, j)
                + SCALE_POWER * SHIFTS[i] * block(i, j + 1)
                + SCALE_POWER * SHIFTS[j] * block(i + 1, j)
                + SCALE_POWER**2 * block(i + 1, j + 1)
            )
        alpha[:, i, DEPTH] = SHIFTS[i] * block(i, 0) + SCALE_POWER * block(i + 1, 0)
    return alpha


ROLLS = range(-8, DEPTH + 1)


def roll_table():
    alpha = moment_terms()
    out = np.zeros((DEPTH * len(ROLLS), LANES), np.float32)
    for i in range(DEPTH):
        for k, d in enumerate(ROLLS):
            for j in range(DEPTH + 1):
                if 0 <= j - d < 9:
                    out[i * len(ROLLS) + k, 8 * j : 8 * j + 8] = alpha[j - d, i, j]
    return out


def pack_kernel(res_ref, diag_ref, out_ref):
    for x in range(CX):
        out_ref[CY * x : CY * x + CY] = jnp.swapaxes(res_ref[:, x], 0, 1)
        out_ref[OWN + x] = diag_ref[x]


def side_kernel(par_ref, own_ref, even_ref, odd_ref, die_ref, link_ref):
    px, core = par_ref[0], par_ref[1]
    first = (DEPTH * (1 - core), DEPTH * core)
    row = lax.broadcasted_iota(jnp.int32, (CY, CZ), 0)
    for ref, base in ((own_ref, DEPTH), (even_ref, 8 * (1 - px)), (odd_ref, 8 * px)):
        for x in range(CX):
            for k in range(DEPTH):
                at = (base + x) * DEPTH + k
                die_ref[at] = ref[CY * x + first[0] + k]
                link_ref[at] = ref[CY * x + first[1] + k]
        for k in range(CX // 2):
            a, b = ref[OWN + 2 * k], ref[OWN + 2 * k + 1]
            top = jnp.where(row < 4, a, pltpu.roll(b, 4, 0))
            bottom = jnp.where(row < 4, pltpu.roll(a, 4, 0), b)
            at = SIDE + base // 2 + k
            die_ref[at] = jnp.where(core == 0, bottom, top)
            link_ref[at] = jnp.where(core == 0, top, bottom)


def basis_kernel(
    par_ref, own_ref, even_ref, odd_ref, die_ref, link_ref, v_ref, gram_ref, e0, e1, e2, e3, dm, bc
):
    px, core = par_ref[0], par_ref[1]
    third = 1.0 / SCALE_POWER
    for ref, base in ((own_ref, DEPTH), (even_ref, 8 * (1 - px)), (odd_ref, 8 * px)):
        for x in range(CX):
            for y in range(CY):
                e0[(base + x) * WY + DEPTH + y] = ref[CY * x + y]
            dm[base + x, DEPTH : DEPTH + CY] = ref[OWN + x]
    for ref, base in ((die_ref, 12 * (1 - core)), (link_ref, 12 * core)):
        for x in range(WX):
            for k in range(DEPTH):
                e0[x * WY + base + k] = ref[x * DEPTH + k]

    for low, high, test in ((link_ref, die_ref, core == 0), (die_ref, link_ref, core == 1)):

        @pl.when(test)
        def _(low=low, high=high):
            for k in range(WX // 2):
                for ref, at in ((low, 0), (high, DEPTH + CY)):
                    dm[2 * k, at : at + DEPTH] = ref[SIDE + k, :DEPTH]
                    dm[2 * k + 1, at : at + DEPTH] = ref[SIDE + k, DEPTH:]

    @pl.loop(1, WY - 1)
    def _(y):
        for x in range(1, WX - 1):
            line = (dm[x, pl.ds(y, 1), :] + (CENTRE + 1.0)) * third
            bc[x * WY + y] = jnp.broadcast_to(line, (NRHS, CZ))

    lane = lax.broadcasted_iota(jnp.int32, (NRHS, LANES), 1)
    scratch = (e0, e1, e2, e3)

    def place(level, x):
        if level and DEPTH <= x < DEPTH + CX:
            return v_ref.at[level - 1], (x - DEPTH) * WY
        return scratch[level], x * WY

    for level, shift in enumerate(SHIFTS):
        margin = level + 1

        @pl.loop(margin, WY - margin)
        def _(y, level=level, shift=shift, margin=margin):
            centre, total = {}, {}
            for x in range(level, WX - level):
                ref, at = place(level, x)
                centre[x] = ref[at + y]
                total[x] = centre[x] + WEIGHT_Y * (ref[at + y - 1] + ref[at + y + 1])
            for x in range(margin, WX - margin):
                t = total[x] + WEIGHT_X * (total[x - 1] + total[x + 1])
                a, b = t[:, :LANES], t[:, LANES:]
                up_a, up_b = pltpu.roll(a, 1, 1), pltpu.roll(b, 1, 1)
                dn_a, dn_b = pltpu.roll(a, LANES - 1, 1), pltpu.roll(b, LANES - 1, 1)
                near_a = jnp.where(lane == 0, 0.0, up_a) + jnp.where(lane == LANES - 1, dn_b, dn_a)
                near_b = jnp.where(lane == 0, up_a, up_b) + jnp.where(lane == LANES - 1, 0.0, dn_b)
                coeff = bc[x * WY + y] - shift * third
                new_a = coeff[:, :LANES] * centre[x][:, :LANES] - third * (a + WEIGHT_Z * near_a)
                new_b = coeff[:, LANES:] * centre[x][:, LANES:] - third * (b + WEIGHT_Z * near_b)
                ref, at = place(level + 1, x)
                ref[at + y, :, :LANES] = new_a
                ref[at + y, :, LANES:] = new_b

        if level < DEPTH - 1:
            zero = jnp.zeros((NRHS, CZ), jnp.float32)

            def clear(xs, ys, level=level):
                @pl.loop(ys[0], ys[1])
                def _(y):
                    for x in range(*xs):
                        ref, at = place(level + 1, x)
                        ref[at + y] = zero

            for index, xs, ys in (
                (2, (margin, DEPTH), (margin, WY - margin)),
                (3, (DEPTH + CX, WX - margin), (margin, WY - margin)),
                (4, (margin, WX - margin), (margin, DEPTH)),
                (5, (margin, WX - margin), (DEPTH + CY, WY - margin)),
            ):
                pl.when(par_ref[index] == 1)(functools.partial(clear, xs, ys))

    def add(x, total):
        for y in range(CY):
            parts = [own_ref[x * CY + y]]
            parts += [v_ref[j, x * WY + DEPTH + y] for j in range(DEPTH)]
            w = jnp.concatenate(parts, 0)
            total += lax.dot_general(
                w, w, (((1,), (1,)), ((), ())), precision=HIGHEST, preferred_element_type=jnp.float32
            )
        return total

    count = (DEPTH + 1) * NRHS
    gram = lax.fori_loop(0, CX, add, jnp.zeros((count, count), jnp.float32))
    gram = jnp.concatenate([gram, jnp.zeros((count, LANES - count), jnp.float32)], 1)
    out = jnp.zeros((NRHS, LANES), jnp.float32)
    for i in range(DEPTH + 1):
        mine = pltpu.roll(gram[8 * i : 8 * i + 8], 8 * i, 1) if i else gram[:8]
        out += jnp.where((lane >= 16 * i - 8) & (lane < 16 * i + 8), mine, 0.0)
    gram_ref[...] = out


def finish_kernel(table_ref, sums_ref, own_ref, v_ref, corr_ref, new_ref, est_ref):
    moments = sums_ref[0]
    for k in range(1, sums_ref.shape[0]):
        moments += sums_ref[k]
    lane = lax.broadcasted_iota(jnp.int32, (NRHS, LANES), 1)
    row = lax.broadcasted_iota(jnp.int32, (NRHS, LANES), 0)
    rolled = [moments if d == 0 else pltpu.roll(moments, (8 * d) % LANES, 1) for d in ROLLS]
    m = []
    for i in range(DEPTH):
        total = jnp.zeros((NRHS, LANES), jnp.float32)
        for k in range(len(ROLLS)):
            total += table_ref[i * len(ROLLS) + k : i * len(ROLLS) + k + 1, :] * rolled[k]
        m.append(total)
    right = list(m)
    for k in range(DEPTH * NRHS):
        i, r = divmod(k, NRHS)
        cols = [jnp.broadcast_to(m[j][:, k : k + 1], (NRHS, LANES)) for j in range(DEPTH)]
        pivot = jnp.broadcast_to(cols[i][r : r + 1, :], (NRHS, LANES))
        line = jnp.broadcast_to(m[i][r : r + 1, :], (NRHS, LANES)) / pivot
        m = [m[j] - cols[j] * line for j in range(DEPTH)]
        m[i] = jnp.where(row == r, line, m[i])
    first = (lane >= 8 * DEPTH) & (lane < 8 * DEPTH + 8)
    c = [jnp.where(first, m[j], 0.0) for j in range(DEPTH)]
    initial = jnp.sum(jnp.where(row == lane, moments, 0.0), 0, keepdims=True)
    initial = pltpu.roll(jnp.broadcast_to(initial, (NRHS, LANES)), 8 * DEPTH, 1)
    gain = right[0] * c[0]
    for j in range(1, DEPTH):
        gain += right[j] * c[j]
    gain = jnp.sum(gain, 0, keepdims=True)
    est = (initial - gain) / initial
    est_ref[...] = est[:1, 8 * DEPTH : 8 * DEPTH + 8]
    rows = []
    for j in range(DEPTH + 1):
        w = jnp.zeros((NRHS, LANES), jnp.float32)
        if j < DEPTH:
            w += SHIFTS[j] * c[j]
        if j:
            w += SCALE_POWER * c[j - 1]
        kept = -pltpu.roll(w, LANES - 24, 1)
        if j == 0:
            kept = jnp.where(lane == row + 8, 1.0, 0.0) + kept
        if j < DEPTH:
            kept = jnp.where(lane < 8, pltpu.roll(c[j], LANES - 32, 1), kept)
        rows.append(kept)
    rows.append(jnp.zeros((LANES - len(rows) * NRHS, LANES), jnp.float32))
    mix = jnp.transpose(jnp.concatenate(rows, 0))[:16, : (DEPTH + 1) * NRHS]
    for x in range(CX):
        parts = []
        for y in range(CY):
            stack = [own_ref[x * CY + y]]
            stack += [v_ref[j, x * WY + DEPTH + y] for j in range(DEPTH)]
            parts.append(
                jnp.dot(
                    mix,
                    jnp.concatenate(stack, 0),
                    precision=HIGHEST,
                    preferred_element_type=jnp.float32,
                )
            )
        both = jnp.stack(parts, 0)
        corr_ref[:, x] = jnp.swapaxes(both[:, :8], 0, 1)
        new_ref[:, x] = jnp.swapaxes(both[:, 8:], 0, 1)


VMEM = pl.BlockSpec(memory_space=pltpu.VMEM)
SMEM = pl.BlockSpec(memory_space=pltpu.SMEM)


def f32(*shape):
    return jax.ShapeDtypeStruct(shape, jnp.float32)


def call(kernel, specs, out_shape, *args, scratch=(), limit=12, flops=10**8):
    return pl.pallas_call(
        kernel,
        in_specs=specs,
        out_specs=jax.tree.map(lambda _: VMEM, out_shape),
        out_shape=out_shape,
        scratch_shapes=scratch,
        cost_estimate=pl.CostEstimate(flops=flops, bytes_accessed=10**6, transcendentals=0),
        compiler_params=pltpu.CompilerParams(vmem_limit_bytes=limit * 2**20),
    )(*args)


def swaps(count, odd):
    out = []
    for i in range(odd, count - 1, 2):
        out += [(i, i + 1), (i + 1, i)]
    return out


def spread(x, axes):
    count = lax.axis_size(axes)
    return lax.all_to_all(jnp.broadcast_to(x[None], (count, *x.shape)), axes, 0, 0, tiled=True)


def body(residual_block, diagonal):
    at_x, at_y = lax.axis_index(GX), lax.axis_index("gy")
    count_x, count_y = lax.axis_size(GX), lax.axis_size("gy")
    par = jnp.stack(
        [
            at_x % 2,
            at_y % 2,
            at_x == 0,
            at_x == count_x - 1,
            at_y == 0,
            at_y == count_y - 1,
        ]
    ).astype(jnp.int32)
    own = call(pack_kernel, [VMEM] * 2, f32(PACK, NRHS, CZ), residual_block, diagonal)
    odd = lax.ppermute(own, GX, swaps(count_x, 1))
    even = lax.ppermute(own, GX, swaps(count_x, 0))
    die, link = call(
        side_kernel, [SMEM] + [VMEM] * 3, [f32(SIDE_PACK, NRHS, CZ)] * 2, par, own, even, odd
    )
    link = lax.ppermute(link, "gy", swaps(count_y, 1))
    die = lax.ppermute(die, "gy", swaps(count_y, 0))
    v, gram = call(
        basis_kernel,
        [SMEM] + [VMEM] * 5,
        [f32(DEPTH, CX * WY, NRHS, CZ), f32(NRHS, LANES)],
        par,
        own,
        even,
        odd,
        die,
        link,
        scratch=[pltpu.VMEM((WX * WY, NRHS, CZ), jnp.float32)] * DEPTH
        + [
            pltpu.VMEM((WX, WY, CZ), jnp.float32),
            pltpu.VMEM((WX * WY, NRHS, CZ), jnp.float32),
        ],
        limit=16,
    )
    sums = spread(spread(gram, NEAR).sum(0), FAR)
    corr, new, est = call(
        finish_kernel,
        [VMEM] * 4,
        [f32(*residual_block.shape), f32(*residual_block.shape), f32(1, NRHS)],
        jnp.asarray(roll_table()),
        sums,
        own,
        v,
    )
    return corr, new, est.reshape(NRHS)


def solution(mesh):
    split = Mesh(mesh.devices.reshape(16, 2, 4, mesh.shape["gy"]), ("z1", "z0", "y", "gy"))
    return jax.shard_map(
        body,
        mesh=split,
        in_specs=(P(None, GX, "gy", None), P(GX, "gy", None)),
        out_specs=(P(None, GX, "gy", None), P(None, GX, "gy", None), P()),
        check_vma=False,
    )
```

time: 205 us -> 111 us (0.54)
  blocking collectives: 136 us -> 61.2 us
  Pallas kernels: 0 us -> 14.4 us
  waiting for transfers between devices: 26.1 us -> 12.6 us
  other arithmetic: 13.1 us -> 0.07 us
  local copies, waits for them, and re-layouts: 10.8 us -> 1.82 us
  starting transfers between devices: 13.5 us -> 19.7 us
  matrix products: 4.96 us -> 0 us
    psum x2 -> x0, blocking collectives: 136 us -> none  [one_axis_at_a_time(): x = lax.psum(x, axis)]
    all_to_all x0 -> x2, blocking collectives: none -> 61.2 us  [spread(): lax.all_to_all(jnp.broadcast_to(x[None], (count, *x.shape)), axes, 0, 0,...]
    pallas_call x0 -> x4, Pallas kernels: none -> 14.4 us  [call(): pl.pallas_call(kernel, in_specs=specs, out_specs=jax.tree.map(lambda _: V...]
    ppermute x4, waiting for transfers between devices: 24.2 us -> 12.6 us  [the longest x1 6.59 us: body(): even = lax.ppermute(own, GX, swaps(count_x, 0))]
    ppermute x4, starting transfers between devices: 10.2 us -> 19.7 us  [the longest x1 10.8 us: body(): link = lax.ppermute(link, 'gy', swaps(count_y, 1))]
    another operation x5 -> x0, other arithmetic: 6.68 us -> none  [the longest x3 3.6 us: solve_small(): factor = jnp.linalg.cholesky(scaled)]
    dot_general x7 -> x0, matrix products: 4.54 us -> none  [the longest x1 1.5 us: body(): lax.dot_general(combined, basis, (((0,), (0,)), ((), ())), precision=high...]
    unnamed x17 -> x6, local copies, waits for them, and re-layouts: 5.73 us -> 1.71 us
  transfers between devices with their start and end apart: 5 -> 4, of which waited for: 5 -> 2; matrix products, arithmetic and copies ran while one was open for 2% -> 0% of each run, Pallas kernels for 0% -> 0%
where the time goes in v1:
time: 111 us; the launch traced here: 110 us
  blocking collectives  61.2 us (55%)
  starting transfers between devices  19.7 us (18%)
  Pallas kernels  14.4 us (13%)
  waiting for transfers between devices  12.6 us (11%)
  local copies, waits for them, and re-layouts  1.82 us (2%)
    all_to_all x2, blocking collectives, spread(): lax.all_to_all(jnp.broadcast_to(x[None], (count, *x.shape)), axes, 0, 0,...  61.2 us
    pallas_call x4, Pallas kernels, call(): pl.pallas_call(kernel, in_specs=specs, out_specs=jax.tree.map(lambda _: V...  14.4 us
    ppermute x1, starting transfers between devices, body(): link = lax.ppermute(link, 'gy', swaps(count_y, 1))  10.8 us
    ppermute x1, waiting for transfers between devices, body(): even = lax.ppermute(own, GX, swaps(count_x, 0))  6.59 us
    ppermute x1, starting transfers between devices, body(): even = lax.ppermute(own, GX, swaps(count_x, 0))  6.29 us
    ppermute x1, waiting for transfers between devices, body(): link = lax.ppermute(link, 'gy', swaps(count_y, 1))  5.96 us
  transfers between devices with their start and end apart: 4, of which 2 were waited for; matrix products, arithmetic and copies ran while one was open for 0% of the time, Pallas kernels for 0%

profile of v1, /device:TPU:2, one launch (start us, length us, event | category | flops | bytes accessed | tf_op | source)
XLA Modules:
  0.0 110.5 jit_solution(9615030216775232351)
XLA Ops:
  0.6 0.0 copy-start
  0.6 0.9 copy-done
  1.6 0.0 copy-start.1
  1.6 0.8 copy-done.1
  2.3 0.1 shard_map.58.own_ref
  2.4 0.0 copy-start.2
  2.4 0.7 collective-permute-start.1
  3.1 6.3 %collective-permute-start = (f32[36,8,256]{2,1,0:T(8,128)S(1)}, f32[36,8,256]{2,1,0:T(8,128)S(1)}, u32[]{:S(2)}, u32[]{:S(2)}) collective-permute-start(f32[36,8,256]{2,1,0:T(8,128)S(1)} %shard_map.58.own_ref), channel_id=1, source_target_pairs={{0,8},{8,0},{16,24},{24,16},{32,40},{40,32},{48,56},{56,48},{64,72... | collective-permute-start | bytes 884744 | tf_op jit(solution)/shard_map/ppermute | solution.py:313
  9.4 0.1 stack.43.par_ref
  9.5 0.0 collective-permute-done.1.odd_ref
  9.5 6.6 %collective-permute-done.even_ref = f32[36,8,256]{2,1,0:T(8,128)S(1)} collective-permute-done((f32[36,8,256]{2,1,0:T(8,128)S(1)}, f32[36,8,256]{2,1,0:T(8,128)S(1)}, u32[]{:S(2)}, u32[]{:S(2)}) %collective-permute-start) | collective-permute-done | bytes 294944 | tf_op jit(solution)/shard_map/ppermute | solution.py:313
  16.1 0.6 shard_map.59
  16.7 1.9 %collective-permute-start.2 = (f32[54,8,256]{2,1,0:T(8,128)S(1)}, f32[54,8,256]{2,1,0:T(8,128)S(1)}, u32[]{:S(2)}, u32[]{:S(2)}) collective-permute-start(f32[54,8,256]{2,1,0:T(8,128)S(1)} %get-tuple-element.10), channel_id=1, source_target_pairs={{0,1},{1,0},{2,3},{3,2},{4,5},{5,4},{6,7},{7,6},{8,9},{9,8},{10,11... | collective-permute-start | bytes 1327112 | tf_op jit(solution)/shard_map/ppermute | solution.py:318
  18.6 10.8 %collective-permute-start.3 = (f32[54,8,256]{2,1,0:T(8,128)S(1)}, f32[54,8,256]{2,1,0:T(8,128)S(1)}, u32[]{:S(2)}, u32[]{:S(2)}) collective-permute-start(f32[54,8,256]{2,1,0:T(8,128)S(1)} %get-tuple-element.11), channel_id=1, source_target_pairs={{1,2},{2,1},{3,4},{4,3},{5,6},{6,5},{9,10},{10,9},{11,12},{12,11},... | collective-permute-start | bytes 1327112 | tf_op jit(solution)/shard_map/ppermute | solution.py:317
  29.4 0.0 collective-permute-done.2.die_ref
  29.4 6.0 %collective-permute-done.3.link_ref = f32[54,8,256]{2,1,0:T(8,128)S(1)} collective-permute-done((f32[54,8,256]{2,1,0:T(8,128)S(1)}, f32[54,8,256]{2,1,0:T(8,128)S(1)}, u32[]{:S(2)}, u32[]{:S(2)}) %collective-permute-start.3) | collective-permute-done | bytes 442400 | tf_op jit(solution)/shard_map/ppermute | solution.py:317
  35.4 7.8 %shard_map.60 = (f32[4,64,8,256]{3,2,1,0:T(8,128)S(1)}, f32[8,128]{1,0:T(8,128)S(1)}) custom-call(s32[6]{0:T(128)S(1)} %stack.43.par_ref, f32[36,8,256]{2,1,0:T(8,128)S(1)} %shard_map.58.own_ref, f32[36,8,256]{2,1,0:T(8,128)S(1)} %collective-permute-done.even_ref, f32[36,8,256]{2,1,0:T(8,128)S(1)} %collective-permute-done.1.odd_ref, ...), custom_call_target="tpu_custom_call" | custom-call | flops 100000000 | bytes 1000000 | tf_op jit(solution)/shard_map/pallas_call | solution.py:275
  43.2 12.4 %all_to_all.10 = f32[64,8,128]{2,1,0:T(8,128)S(1)} all-to-all(f32[64,8,128]{2,1,0:T(8,128)S(1)} %broadcast_in_dim.4), channel_id=1, replica_groups=mesh['z1'=16,'z0'=2,'y'=4,'gy'=8] {'z0','y','gy'}, dimensions={0} | all-to-all | bytes 524288 | tf_op jit(solution)/shard_map/all_to_all | solution.py:295
  55.6 0.1 reduce_sum.9
  55.7 48.8 %all_to_all.11.sums_ref = f32[16,8,128]{2,1,0:T(8,128)S(1)} all-to-all(f32[16,8,128]{2,1,0:T(8,128)S(1)} %broadcast_in_dim.5), channel_id=1, replica_groups=mesh['z1'=16,'z0'=2,'y'=4,'gy'=8] {'z1'}, dimensions={0} | all-to-all | bytes 131072 | tf_op jit(solution)/shard_map/all_to_all | solution.py:295
  104.5 0.0 copy-done.2
  104.5 6.0 %shard_map.61 = (f32[8,4,8,256]{3,2,1,0:T(8,128)}, f32[8,4,8,256]{3,2,1,0:T(8,128)}, f32[1,8]{1,0:T(1,128)}) custom-call(f32[52,128]{1,0:T(8,128)S(1)} %copy-done.2, f32[16,8,128]{2,1,0:T(8,128)S(1)} %all_to_all.11.sums_ref, f32[36,8,256]{2,1,0:T(8,128)S(1)} %shard_map.58.own_ref, f32[4,64,8,256]{3,2,1,0:T(8,128)S(1)} %get-tuple-element.13.v_ref), custom_call_target="tpu_custom_call" | custom-call | flops 100000000 | bytes 1000000 | tf_op jit(solution)/shard_map/pallas_call | solution.py:275
  (2 shorter events, 0.0 us)
Async XLA Ops:
  0.6 1.0 copy-start
  1.6 0.8 copy-start.1
  2.4 102.1 %copy-start.2 = (f32[52,128]{1,0:T(8,128)S(1)}, f32[52,128]{1,0:T(8,128)}, u32[]{:S(2)}) copy-start(f32[52,128]{1,0:T(8,128)} %constant.50.clone.table_ref) | copy-start | bytes 79876
  2.4 7.1 %collective-permute-start.1 = (f32[36,8,256]{2,1,0:T(8,128)S(1)}, f32[36,8,256]{2,1,0:T(8,128)S(1)}, u32[]{:S(2)}, u32[]{:S(2)}) collective-permute-start(f32[36,8,256]{2,1,0:T(8,128)S(1)} %shard_map.58.own_ref), channel_id=1, source_target_pairs={{8,16},{16,8},{24,32},{32,24},{40,48},{48,40},{56,64},{64,56},{72,... | collective-permute-start | bytes 884744 | tf_op jit(solution)/shard_map/ppermute | solution.py:312
  3.1 13.0 %collective-permute-start = (f32[36,8,256]{2,1,0:T(8,128)S(1)}, f32[36,8,256]{2,1,0:T(8,128)S(1)}, u32[]{:S(2)}, u32[]{:S(2)}) collective-permute-start(f32[36,8,256]{2,1,0:T(8,128)S(1)} %shard_map.58.own_ref), channel_id=1, source_target_pairs={{0,8},{8,0},{16,24},{24,16},{32,40},{40,32},{48,56},{56,48},{64,72... | collective-permute-start | bytes 884744 | tf_op jit(solution)/shard_map/ppermute | solution.py:313
  16.7 12.7 %collective-permute-start.2 = (f32[54,8,256]{2,1,0:T(8,128)S(1)}, f32[54,8,256]{2,1,0:T(8,128)S(1)}, u32[]{:S(2)}, u32[]{:S(2)}) collective-permute-start(f32[54,8,256]{2,1,0:T(8,128)S(1)} %get-tuple-element.10), channel_id=1, source_target_pairs={{0,1},{1,0},{2,3},{3,2},{4,5},{5,4},{6,7},{7,6},{8,9},{9,8},{10,11... | collective-permute-start | bytes 1327112 | tf_op jit(solution)/shard_map/ppermute | solution.py:318
  18.6 16.8 %collective-permute-start.3 = (f32[54,8,256]{2,1,0:T(8,128)S(1)}, f32[54,8,256]{2,1,0:T(8,128)S(1)}, u32[]{:S(2)}, u32[]{:S(2)}) collective-permute-start(f32[54,8,256]{2,1,0:T(8,128)S(1)} %get-tuple-element.11), channel_id=1, source_target_pairs={{1,2},{2,1},{3,4},{4,3},{5,6},{6,5},{9,10},{10,9},{11,12},{12,11},... | collective-permute-start | bytes 1327112 | tf_op jit(solution)/shard_map/ppermute | solution.py:317

commit v2 on v1

v2 whole, which is shorter than its diff:
```python
import jax
import jax.numpy as jnp
import numpy as np
from jax import lax
from jax.experimental import pallas as pl
from jax.experimental.pallas import tpu as pltpu
from jax.sharding import Mesh
from jax.sharding import PartitionSpec as P

NRHS = 8
WEIGHT_X = 0.4
WEIGHT_Y = 0.2
WEIGHT_Z = 0.1
CENTRE = 2.2
SCALE_POWER = 3.0
THIRD = 1.0 / SCALE_POWER
SHIFTS = (6.0, 1.5, 4.5, 3.0)
DEPTH = len(SHIFTS)

CX, CY, CZ = 4, 8, 256
WX, WY = CX + 2 * DEPTH, CY + 2 * DEPTH
LANES = 128

GX = ("z1", "z0", "y")
NEAR = ("z0", "y", "gy")
FAR = ("z1",)
OWN = CX * CY
PACK = OWN + CX
NEXT = CX * DEPTH + CX // 2
REST = 2 * CX * DEPTH + CX
BLOCKS = 2 * DEPTH + 1
USED = BLOCKS * NRHS
MESSAGE = 3 * LANES


def moment_terms():
    table = {}
    for j in range(DEPTH + 1):
        for i in (j, j + 1):
            if i <= DEPTH:
                table[i, j] = np.eye(BLOCKS)[2 * j + (i - j)]
    for gap in range(2, DEPTH + 1):
        for j in range(DEPTH + 1 - gap):
            i = j + gap - 1
            low = table[i, j + 1]
            table[i + 1, j] = low + (SHIFTS[j] - SHIFTS[i]) / SCALE_POWER * table[i, j]

    def block(i, j):
        return table[max(i, j), min(i, j)]

    alpha = np.zeros((BLOCKS, DEPTH, DEPTH + 1))
    for i in range(DEPTH):
        for j in range(DEPTH):
            alpha[:, i, j] = (
                SHIFTS[i] * SHIFTS[j] * block(i, j)
                + SCALE_POWER * SHIFTS[i] * block(i, j + 1)
                + SCALE_POWER * SHIFTS[j] * block(i + 1, j)
                + SCALE_POWER**2 * block(i + 1, j + 1)
            )
        alpha[:, i, DEPTH] = SHIFTS[i] * block(i, 0) + SCALE_POWER * block(i + 1, 0)
    return alpha


ROLLS = range(1 - BLOCKS, DEPTH)


def roll_table():
    alpha = moment_terms()
    out = np.zeros(((DEPTH + 1) * len(ROLLS), LANES), np.float32)
    for j in range(DEPTH + 1):
        for k, d in enumerate(ROLLS):
            for i in range(DEPTH):
                if 0 <= i - d < BLOCKS:
                    out[j * len(ROLLS) + k, 8 * i : 8 * i + 8] = alpha[i - d, i, j]
    return out


def iota(axis):
    return lax.broadcasted_iota(jnp.int32, (NRHS, LANES), axis)


def spin(x, by):
    by %= LANES
    return pltpu.roll(x, by, 1) if by else x


def halves(a, b, first):
    low = lax.broadcasted_iota(jnp.int32, (CY, CZ), 0) < DEPTH
    if first:
        return jnp.where(low, pltpu.roll(a, DEPTH, 0), b)
    return jnp.where(low, a, pltpu.roll(b, DEPTH, 0))


def pack_kernel(par_ref, res_hbm, diag_hbm, out_ref, next_ref, res_ref, diag_ref, sems):
    core = par_ref[1]
    copies = (
        pltpu.make_async_copy(res_hbm, res_ref, sems.at[0]),
        pltpu.make_async_copy(diag_hbm, diag_ref, sems.at[1]),
    )
    for copy in copies:
        copy.start()
    for copy in copies:
        copy.wait()
    for x in range(CX):
        out_ref[CY * x : CY * x + CY] = jnp.swapaxes(res_ref[:, x], 0, 1)
        out_ref[OWN + x] = diag_ref[x]
    first = DEPTH * core
    for x in range(CX):
        for k in range(DEPTH):
            next_ref[DEPTH * x + k] = out_ref[CY * x + first + k]
    for k in range(CX // 2):
        a, b = diag_ref[2 * k], diag_ref[2 * k + 1]
        next_ref[CX * DEPTH + k] = jnp.where(core == 0, halves(a, b, 0), halves(a, b, DEPTH))


def side_kernel(par_ref, own_ref, even_ref, odd_ref, next_ref, die_ref, link_ref):
    del next_ref
    px, core = par_ref[0], par_ref[1]
    sides = ((own_ref, CX), (even_ref, 2 * CX * (1 - px)), (odd_ref, 2 * CX * px))
    for which, (ref, base) in enumerate(sides):
        packed = base // 2 if which else 0
        for x in range(CX):
            for k in range(DEPTH):
                die_ref[(base + x) * DEPTH + k] = ref[CY * x + DEPTH * (1 - core) + k]
                if which:
                    link_ref[(packed + x) * DEPTH + k] = ref[CY * x + DEPTH * core + k]
        for k in range(CX // 2):
            a, b = ref[OWN + 2 * k], ref[OWN + 2 * k + 1]
            low, high = halves(a, b, 0), halves(a, b, DEPTH)
            die_ref[WX * DEPTH + base // 2 + k] = jnp.where(core == 0, high, low)
            if which:
                link_ref[2 * CX * DEPTH + packed // 2 + k] = jnp.where(core == 0, low, high)


def place(e_ref, v_ref, level, x):
    if level and DEPTH <= x < DEPTH + CX:
        return v_ref.at[level - 1], (x - DEPTH) * WY
    return e_ref.at[level], x * WY


def advance(e_ref, v_ref, bc_ref, level, rows):
    margin = level + 1
    lane = iota(1)
    for y in rows:
        centre, total = {}, {}
        for x in range(level, WX - level):
            ref, at = place(e_ref, v_ref, level, x)
            centre[x] = ref[at + y]
            total[x] = centre[x] + WEIGHT_Y * (ref[at + y - 1] + ref[at + y + 1])
        for x in range(margin, WX - margin):
            t = total[x] + WEIGHT_X * (total[x - 1] + total[x + 1])
            a, b = t[:, :LANES], t[:, LANES:]
            up_a, up_b = spin(a, 1), spin(b, 1)
            dn_a, dn_b = spin(a, -1), spin(b, -1)
            near_a = jnp.where(lane == 0, 0.0, up_a) + jnp.where(lane == LANES - 1, dn_b, dn_a)
            near_b = jnp.where(lane == 0, up_a, up_b) + jnp.where(lane == LANES - 1, 0.0, dn_b)
            coeff = bc_ref[x * WY + y] - SHIFTS[level] * THIRD
            ref, at = place(e_ref, v_ref, level + 1, x)
            ref[at + y, :, :LANES] = coeff[:, :LANES] * centre[x][:, :LANES] - THIRD * (
                a + WEIGHT_Z * near_a
            )
            ref[at + y, :, LANES:] = coeff[:, LANES:] * centre[x][:, LANES:] - THIRD * (
                b + WEIGHT_Z * near_b
            )


def clear(e_ref, v_ref, level, xs, ys):
    zero = jnp.zeros((NRHS, CZ), jnp.float32)

    @pl.loop(ys[0], ys[1])
    def _(y):
        for x in range(*xs):
            ref, at = place(e_ref, v_ref, level, x)
            ref[at + y] = zero


def clear_planes(par_ref, e_ref, v_ref, level, spans):
    for index, xs in ((2, (level, DEPTH)), (3, (DEPTH + CX, WX - level))):

        @pl.when(par_ref[index] == 1)
        def _(xs=xs):
            for ys in spans:
                clear(e_ref, v_ref, level, xs, ys)


def scaled(line):
    return jnp.broadcast_to((line + (CENTRE + 1.0)) * THIRD, (NRHS, CZ))


def inner_kernel(par_ref, own_ref, even_ref, odd_ref, e_ref, v_ref, bc_ref):
    px = par_ref[0]
    for ref, base in ((own_ref, CX), (even_ref, 2 * CX * (1 - px)), (odd_ref, 2 * CX * px)):
        for x in range(CX):
            for y in range(CY):
                at = (base + x) * WY + DEPTH + y
                e_ref[0, at] = ref[CY * x + y]
                bc_ref[at] = scaled(ref[OWN + x, y : y + 1])
    for level in range(DEPTH - 1):
        low, high = DEPTH + level + 1, DEPTH + CY - level - 1
        advance(e_ref, v_ref, bc_ref, level, range(low, high))
        clear_planes(par_ref, e_ref, v_ref, level + 1, ((low, high),))


def split(a):
    high = a.astype(jnp.bfloat16).astype(jnp.float32)
    rest = a - high
    middle = rest.astype(jnp.bfloat16).astype(jnp.float32)
    return high, middle, rest - middle


def basis_kernel(
    par_ref, own_ref, next_ref, link_ref, die_ref, e_in, v_in, bc_in, e_ref, v_ref, bc_ref, out_ref
):
    del e_in, v_in, bc_in
    core = par_ref[1]
    die_at, link_at = 3 * DEPTH * (1 - core), 3 * DEPTH * core
    sources = [(die_ref, x, x, WX, die_at) for x in range(WX)]
    sources += [(next_ref, x, CX + x, CX, link_at) for x in range(CX)]
    sources += [(link_ref, x, x if x < CX else CX + x, 2 * CX, link_at) for x in range(2 * CX)]
    for ref, mine, x, count, base in sources:
        for k in range(DEPTH):
            at = x * WY + base + k
            e_ref[0, at] = ref[mine * DEPTH + k]
            row = DEPTH * (mine % 2) + k
            bc_ref[at] = scaled(ref[count * DEPTH + mine // 2, row : row + 1])
    for level in range(DEPTH):
        m = level + 1
        low, high = DEPTH + m, DEPTH + CY - m
        if low >= high:
            rows = (range(m, WY - m),)
        else:
            rows = (range(m, low), range(high, WY - m))
        for part in rows:
            advance(e_ref, v_ref, bc_ref, level, part)
        if m < DEPTH:
            clear_planes(par_ref, e_ref, v_ref, m, [(part[0], part[-1] + 1) for part in rows])
            for index, ys in ((4, (m, DEPTH)), (5, (DEPTH + CY, WY - m))):

                @pl.when(par_ref[index] == 1)
                def _(ys=ys, m=m):
                    clear(e_ref, v_ref, m, (m, WX - m), ys)

    def add(x, total):
        for y in range(CY):
            parts = [split(own_ref[x * CY + y])]
            parts += [split(v_ref[j, x * WY + DEPTH + y]) for j in range(DEPTH)]
            stack = [part[k] for k in range(3) for part in parts]
            stack.append(jnp.zeros((NRHS, CZ), jnp.float32))
            w = jnp.concatenate(stack, 0).astype(jnp.bfloat16)
            total += lax.dot_general(
                w, w, (((1,), (1,)), ((), ())), preferred_element_type=jnp.float32
            )
        return total

    gram = lax.fori_loop(0, CX, add, jnp.zeros((LANES, LANES), jnp.float32))
    lane, row = iota(1), iota(0)
    moments = jnp.zeros((NRHS, LANES), jnp.float32)
    count = (DEPTH + 1) * NRHS
    for i in range(DEPTH + 1):
        mine = sum(gram[k * count + 8 * i : k * count + 8 * i + 8] for k in range(3))
        mine = spin(mine, 8 * i) + spin(mine, 8 * i - count) + spin(mine, 8 * i - 2 * count)
        moments += jnp.where((lane >= 16 * i - 8) & (lane < 16 * i + 8), mine, 0.0)
    turn = [
        jnp.sum(jnp.where(row == ((lane - k) & 7), moments, 0.0), 0, keepdims=True)
        for k in range(5)
    ]
    at = lane[:1]
    out_ref[:, :LANES] = jnp.where(at < USED, turn[0], spin(turn[3], USED))
    out_ref[:, LANES : 2 * LANES] = jnp.where(
        at < USED, turn[1], jnp.where(at < 88, spin(turn[3], 16), spin(turn[4], 88))
    )
    out_ref[:, 2 * LANES :] = jnp.where(at < USED, turn[2], spin(turn[4], 32))


def unpack(sums):
    at, lane, row = iota(1)[:1], iota(1), iota(0)
    a, b, c = sums[:, :LANES], sums[:, LANES : 2 * LANES], sums[:, 2 * LANES :]
    turn = [a, b, c]
    turn.append(jnp.where(at < 56, spin(a, 56), spin(b, -16)))
    turn.append(jnp.where(at < 40, spin(b, 40), spin(c, -32)))
    for k in (5, 6, 7):
        j = 8 - k
        turn.append(jnp.where((at & 7) + j < 8, spin(turn[j], -j), spin(turn[j], 8 - j)))
    moments = jnp.zeros((NRHS, LANES), jnp.float32)
    for k in range(8):
        moments += jnp.where(
            (((lane - row) & 7) == k) & (lane < USED),
            jnp.broadcast_to(turn[k], (NRHS, LANES)),
            0.0,
        )
    return moments


def solve(table_ref, moments):
    lane = iota(1)
    rolled = [spin(moments, 8 * d) for d in ROLLS]
    a = []
    for j in range(DEPTH + 1):
        total = jnp.zeros((NRHS, LANES), jnp.float32)
        for k in range(len(ROLLS)):
            at = j * len(ROLLS) + k
            total += table_ref[at : at + 1, :] * rolled[k]
        a.append(total)
    right = a[DEPTH]
    for q in range(DEPTH):
        live = range(q, DEPTH + 1)
        col = [
            {j: jnp.broadcast_to(a[j][:, 8 * q + c : 8 * q + c + 1], (NRHS, LANES)) for j in live}
            for c in range(NRHS)
        ]
        for c in range(NRHS):
            k = 8 * q + c
            inverse = 1.0 / jnp.broadcast_to(col[c][q][c : c + 1], (NRHS, LANES))
            line = jnp.broadcast_to(a[q][c : c + 1], (NRHS, LANES)) * inverse
            for j in live:
                a[j] = jnp.where(lane == k, col[c][j] * inverse, a[j] - col[c][j] * line)
            for d in range(c + 1, NRHS):
                factor = jnp.broadcast_to(col[d][q][c : c + 1], (NRHS, LANES)) * inverse
                for j in live:
                    col[d][j] = col[d][j] - col[c][j] * factor
    return jnp.where(lane < DEPTH * NRHS, a[DEPTH], 0.0), right


def finish_kernel(table_ref, sums_ref, own_ref, v_ref, corr_ref, new_ref, est_ref):
    sums = sums_ref[0]
    for k in range(1, sums_ref.shape[0]):
        sums += sums_ref[k]
    moments = unpack(sums)
    lane, row = iota(1), iota(0)
    coeffs, right = solve(table_ref, moments)
    initial = jnp.sum(jnp.where(lane == row, moments, 0.0), 1, keepdims=True)
    gain = jnp.sum(right * coeffs, 1, keepdims=True)
    est = jnp.broadcast_to((initial - gain) / initial, (NRHS, LANES))
    est = jnp.sum(jnp.where(lane == row, est, 0.0), 0, keepdims=True)
    est_ref[...] = est[:, :NRHS]
    shift = jnp.zeros((NRHS, LANES), jnp.float32)
    for j in range(DEPTH):
        shift = jnp.where((lane >= 8 * j) & (lane < 8 * j + 8), SHIFTS[j], shift)
    kept = jnp.where(lane == row, 1.0, 0.0) - (shift * coeffs + SCALE_POWER * spin(coeffs, 8))
    high, middle, low = split(jnp.concatenate([coeffs, kept], 0))
    lane = lax.broadcasted_iota(jnp.int32, (2 * NRHS, LANES), 1)
    count = (DEPTH + 1) * NRHS
    middle_at = spin(middle, 3 * count)
    first = high + spin(high, count) + spin(high, 2 * count)
    first += jnp.where(lane >= 3 * count, middle_at, 0.0)
    second = jnp.where(lane < 4 * count - LANES, middle_at, 0.0)
    second += spin(middle, 4 * count) + spin(low, 5 * count)
    mix = jnp.concatenate([first, second], 1).astype(jnp.bfloat16)
    for x in range(CX):
        parts = []
        for y in range(CY):
            terms = [split(own_ref[x * CY + y])]
            terms += [split(v_ref[j, x * WY + DEPTH + y]) for j in range(DEPTH)]
            stack = [term[k] for k in (0, 1, 2, 0, 1, 0) for term in terms]
            stack += [jnp.zeros((NRHS, CZ), jnp.float32)] * 2
            w = jnp.concatenate(stack, 0).astype(jnp.bfloat16)
            parts.append(jnp.dot(mix, w, preferred_element_type=jnp.float32))
        both = jnp.stack(parts, 0)
        corr_ref[:, x] = jnp.swapaxes(both[:, :NRHS], 0, 1)
        new_ref[:, x] = jnp.swapaxes(both[:, NRHS:], 0, 1)


VMEM = pl.BlockSpec(memory_space=pltpu.VMEM)
SMEM = pl.BlockSpec(memory_space=pltpu.SMEM)
HBM = pl.BlockSpec(memory_space=pltpu.HBM)


def f32(*shape):
    return jax.ShapeDtypeStruct(shape, jnp.float32)


def call(kernel, specs, out_shape, *args, scratch=(), limit=12, flops=10**8, aliases=None):
    return pl.pallas_call(
        kernel,
        in_specs=specs,
        out_specs=jax.tree.map(lambda _: VMEM, out_shape),
        out_shape=out_shape,
        scratch_shapes=scratch,
        input_output_aliases=aliases or {},
        cost_estimate=pl.CostEstimate(flops=flops, bytes_accessed=10**6, transcendentals=0),
        compiler_params=pltpu.CompilerParams(vmem_limit_bytes=limit * 2**20),
    )(*args)


def swaps(count, odd):
    out = []
    for i in range(odd, count - 1, 2):
        out += [(i, i + 1), (i + 1, i)]
    return out


def spread(x, axes, groups=None):
    count = lax.axis_size(axes)
    copies = jnp.broadcast_to(x[None], (count, *x.shape))
    return lax.all_to_all(copies, axes, 0, 0, tiled=True, axis_index_groups=groups)


def body(residual_block, diagonal):
    at_x, at_y = lax.axis_index(GX), lax.axis_index("gy")
    count_x, count_y = lax.axis_size(GX), lax.axis_size("gy")
    par = jnp.stack(
        [
            at_x & 1,
            at_y & 1,
            at_x == 0,
            at_x == count_x - 1,
            at_y == 0,
            at_y == count_y - 1,
        ]
    ).astype(jnp.int32)
    own, nxt = call(
        pack_kernel,
        [SMEM, HBM, HBM],
        [f32(PACK, NRHS, CZ), f32(NEXT, NRHS, CZ)],
        par,
        residual_block,
        diagonal,
        scratch=[
            pltpu.VMEM(residual_block.shape, jnp.float32),
            pltpu.VMEM(diagonal.shape, jnp.float32),
            pltpu.SemaphoreType.DMA((2,)),
        ],
    )
    odd = lax.ppermute(own, GX, swaps(count_x, 1))
    even = lax.ppermute(own, GX, swaps(count_x, 0))
    nxt = lax.ppermute(nxt, "gy", swaps(count_y, 1))
    die, link = call(
        side_kernel,
        [SMEM] + [VMEM] * 4,
        [f32(WX * DEPTH + WX // 2, NRHS, CZ), f32(REST, NRHS, CZ)],
        par,
        own,
        even,
        odd,
        nxt,
    )
    link = lax.ppermute(link, "gy", swaps(count_y, 1))
    die = lax.ppermute(die, "gy", swaps(count_y, 0))
    state = [
        f32(DEPTH, WX * WY, NRHS, CZ),
        f32(DEPTH, CX * WY, NRHS, CZ),
        f32(WX * WY, NRHS, CZ),
    ]
    e, v, bc = call(inner_kernel, [SMEM] + [VMEM] * 3, state, par, own, even, odd)
    e, v, bc, message = call(
        basis_kernel,
        [SMEM] + [VMEM] * 7,
        [*state, f32(1, MESSAGE)],
        par,
        own,
        nxt,
        link,
        die,
        e,
        v,
        bc,
        aliases={5: 0, 6: 1, 7: 2},
    )
    count = lax.axis_size(FAR)
    order = [[(count // 2 + i) % count for i in range(count)]]
    sums = spread(spread(message, NEAR).sum(0), FAR, order)
    corr, new, est = call(
        finish_kernel,
        [VMEM] * 4,
        [f32(*residual_block.shape), f32(*residual_block.shape), f32(1, NRHS)],
        jnp.asarray(roll_table()),
        sums,
        own,
        v,
    )
    return corr, new, est.reshape(NRHS)


def solution(mesh):
    split_mesh = Mesh(mesh.devices.reshape(16, 2, 4, mesh.shape["gy"]), ("z1", "z0", "y", "gy"))
    return jax.shard_map(
        body,
        mesh=split_mesh,
        in_specs=(P(None, GX, "gy", None), P(GX, "gy", None)),
        out_specs=(P(None, GX, "gy", None), P(None, GX, "gy", None), P()),
        check_vma=False,
    )
```

time: 111 us -> 88.3 us (0.80)
  the two profiles are of different devices: /device:TPU:2 before, /device:TPU:1 now
where the time goes in v2:
time: 88.3 us; the launch traced here: 88 us
  blocking collectives  44.4 us (50%)
  starting transfers between devices  24.4 us (28%)
  Pallas kernels  8.93 us (10%)
  waiting for transfers between devices  7.48 us (8%)
  local copies, waits for them, and re-layouts  1.87 us (2%)
    all_to_all x2, blocking collectives, spread(): lax.all_to_all(copies, axes, 0, 0, tiled=True, axis_index_groups=groups)  44.4 us
    ppermute x1, starting transfers between devices, body(): die = lax.ppermute(die, 'gy', swaps(count_y, 0))  11 us
    pallas_call x5, Pallas kernels, call(): pl.pallas_call(kernel, in_specs=specs, out_specs=jax.tree.map(lambda _: V...  8.93 us
    ppermute x1, starting transfers between devices, body(): even = lax.ppermute(own, GX, swaps(count_x, 0))  6.55 us
    ppermute x1, waiting for transfers between devices, body(): link = lax.ppermute(link, 'gy', swaps(count_y, 1))  4.66 us
    ppermute x1, starting transfers between devices, body(): nxt = lax.ppermute(nxt, 'gy', swaps(count_y, 1))  4.24 us
    ppermute x1, waiting for transfers between devices, body(): nxt = lax.ppermute(nxt, 'gy', swaps(count_y, 1))  2.81 us
    ppermute x1, starting transfers between devices, body(): link = lax.ppermute(link, 'gy', swaps(count_y, 1))  1.92 us
  transfers between devices with their start and end apart: 5, of which 2 were waited for; matrix products, arithmetic and copies ran while one was open for 0% of the time, Pallas kernels for 2%

profile of v2, /device:TPU:1, one launch (start us, length us, event | category | flops | bytes accessed | tf_op | source)
XLA Modules:
  0.0 88.0 jit_solution(4228263491018299812)
XLA Ops:
  0.6 0.1 stack.43.par_ref
  0.7 0.0 copy-start.1
  0.7 1.0 %copy-done.1 = f32[8,4,8,256]{3,2,1,0:T(8,128)S(1)} copy-done((f32[8,4,8,256]{3,2,1,0:T(8,128)S(1)}, f32[8,4,8,256]{3,2,1,0:T(8,128)}, u32[]{:S(2)}) %copy-start.1) | copy-done | bytes 262168
  1.7 0.0 copy-start.2
  1.7 0.8 copy-done.2
  2.4 0.7 shard_map.58
  3.1 0.7 collective-permute-start.2
  3.8 6.5 %collective-permute-start.1 = (f32[36,8,256]{2,1,0:T(8,128)S(1)}, f32[36,8,256]{2,1,0:T(8,128)S(1)}, u32[]{:S(2)}, u32[]{:S(2)}) collective-permute-start(f32[36,8,256]{2,1,0:T(8,128)S(1)} %get-tuple-element.15.own_ref), channel_id=1, source_target_pairs={{0,8},{8,0},{16,24},{24,16},{32,40},{40,32},{48,56},{56,48},{64,72... | collective-permute-start | bytes 884744 | tf_op jit(solution)/shard_map/ppermute | solution.py:425
  10.4 4.2 %collective-permute-start = (f32[18,8,256]{2,1,0:T(8,128)S(1)}, f32[18,8,256]{2,1,0:T(8,128)S(1)}, u32[]{:S(2)}, u32[]{:S(2)}) collective-permute-start(f32[18,8,256]{2,1,0:T(8,128)S(1)} %get-tuple-element.16), channel_id=1, source_target_pairs={{1,2},{2,1},{3,4},{4,3},{5,6},{6,5},{9,10},{10,9},{11,12},{12,11},... | collective-permute-start | bytes 442376 | tf_op jit(solution)/shard_map/ppermute | solution.py:426
  14.6 2.8 %collective-permute-done.next_ref = f32[18,8,256]{2,1,0:T(8,128)S(1)} collective-permute-done((f32[18,8,256]{2,1,0:T(8,128)S(1)}, f32[18,8,256]{2,1,0:T(8,128)S(1)}, u32[]{:S(2)}, u32[]{:S(2)}) %collective-permute-start) | collective-permute-done | bytes 147488 | tf_op jit(solution)/shard_map/ppermute | solution.py:426
  17.4 0.0 collective-permute-done.2.odd_ref
  17.4 0.0 collective-permute-done.1.even_ref
  17.4 0.6 shard_map.59
  18.1 11.0 %collective-permute-start.4 = (f32[54,8,256]{2,1,0:T(8,128)S(1)}, f32[54,8,256]{2,1,0:T(8,128)S(1)}, u32[]{:S(2)}, u32[]{:S(2)}) collective-permute-start(f32[54,8,256]{2,1,0:T(8,128)S(1)} %get-tuple-element.18), channel_id=1, source_target_pairs={{0,1},{1,0},{2,3},{3,2},{4,5},{5,4},{6,7},{7,6},{8,9},{9,8},{10,11... | collective-permute-start | bytes 1327112 | tf_op jit(solution)/shard_map/ppermute | solution.py:438
  29.1 1.9 %collective-permute-start.3 = (f32[36,8,256]{2,1,0:T(8,128)S(1)}, f32[36,8,256]{2,1,0:T(8,128)S(1)}, u32[]{:S(2)}, u32[]{:S(2)}) collective-permute-start(f32[36,8,256]{2,1,0:T(8,128)S(1)} %get-tuple-element.17), channel_id=1, source_target_pairs={{1,2},{2,1},{3,4},{4,3},{5,6},{6,5},{9,10},{10,9},{11,12},{12,11},... | collective-permute-start | bytes 884744 | tf_op jit(solution)/shard_map/ppermute | solution.py:437
  31.0 1.4 %shard_map.60 = (f32[4,192,8,256]{3,2,1,0:T(8,128)S(1)}, f32[4,64,8,256]{3,2,1,0:T(8,128)S(1)}, f32[192,8,256]{2,1,0:T(8,128)S(1)}) custom-call(s32[6]{0:T(128)S(1)} %stack.43.par_ref, f32[36,8,256]{2,1,0:T(8,128)S(1)} %get-tuple-element.15.own_ref, f32[36,8,256]{2,1,0:T(8,128)S(1)} %collective-permute-done.1.even_ref, ...), custom_call_target="tpu_custom_call" | custom-call | flops 100000000 | bytes 1000000 | tf_op jit(solution)/shard_map/pallas_call | solution.py:373
  32.5 4.7 %collective-permute-done.3.link_ref = f32[36,8,256]{2,1,0:T(8,128)S(1)} collective-permute-done((f32[36,8,256]{2,1,0:T(8,128)S(1)}, f32[36,8,256]{2,1,0:T(8,128)S(1)}, u32[]{:S(2)}, u32[]{:S(2)}) %collective-permute-start.3) | collective-permute-done | bytes 294944 | tf_op jit(solution)/shard_map/ppermute | solution.py:437
  37.1 0.0 collective-permute-done.4.die_ref
  37.1 0.0 copy-start
  37.1 3.6 %shard_map.61 = (f32[4,192,8,256]{3,2,1,0:T(8,128)S(1)}, f32[4,64,8,256]{3,2,1,0:T(8,128)S(1)}, f32[192,8,256]{2,1,0:T(8,128)S(1)}, f32[1,384]{1,0:T(1,128)S(1)}) custom-call(s32[6]{0:T(128)S(1)} %stack.43.par_ref, f32[36,8,256]{2,1,0:T(8,128)S(1)} %get-tuple-element.15.own_ref, ...), custom_call_target="tpu_custom_call", output_to_operand_aliasing={{0}: (5, {}), {1}: (6, {}), {2}: (7, {})} | custom-call | flops 100000000 | bytes 1000000 | tf_op jit(solution)/shard_map/pallas_call | solution.py:373
  40.7 0.1 broadcast_in_dim.7
  40.8 10.4 %all_to_all.10 = f32[64,1,384]{2,1,0:T(1,128)S(1)} all-to-all(f32[64,1,384]{2,1,0:T(1,128)S(1)} %broadcast_in_dim.7), channel_id=1, replica_groups=mesh['z1'=16,'z0'=2,'y'=4,'gy'=8] {'z0','y','gy'}, dimensions={0} | all-to-all | bytes 196608 | tf_op jit(solution)/shard_map/all_to_all | solution.py:395
  51.2 0.1 reduce_sum.9
  51.3 34.0 %all_to_all.11.sums_ref = f32[16,1,384]{2,1,0:T(1,128)S(1)} all-to-all(f32[16,1,384]{2,1,0:T(1,128)S(1)} %broadcast_in_dim.16), channel_id=1, replica_groups={{512,576,640,704,768,832,896,960,0,64,128,192,256,320,384,448},{513,577..., dimensions={0} | all-to-all | bytes 49152 | tf_op jit(solution)/shard_map/all_to_all | solution.py:395
  85.3 0.0 copy-done
  85.3 2.6 %shard_map.62 = (f32[8,4,8,256]{3,2,1,0:T(8,128)}, f32[8,4,8,256]{3,2,1,0:T(8,128)}, f32[1,8]{1,0:T(1,128)}) custom-call(f32[60,128]{1,0:T(8,128)S(1)} %copy-done, f32[16,1,384]{2,1,0:T(1,128)S(1)} %all_to_all.11.sums_ref, f32[36,8,256]{2,1,0:T(8,128)S(1)} %get-tuple-element.15.own_ref, f32[4,64,8,256]{3,2,1,0:T(8,128)S(1)} %get-tuple-element.23.v_ref), custom_call_target="tpu_custom_call" | custom-call | flops 100000000 | bytes 1000000 | tf_op jit(solution)/shard_map/pallas_call | solution.py:373
  (2 shorter events, 0.0 us)
Async XLA Ops:
  0.7 1.0 %copy-start.1 = (f32[8,4,8,256]{3,2,1,0:T(8,128)S(1)}, f32[8,4,8,256]{3,2,1,0:T(8,128)}, u32[]{:S(2)}) copy-start(f32[8,4,8,256]{3,2,1,0:T(8,128)} %res_hbm.1) | copy-start | bytes 786436
  1.7 0.8 copy-start.2
  3.1 14.3 %collective-permute-start.2 = (f32[36,8,256]{2,1,0:T(8,128)S(1)}, f32[36,8,256]{2,1,0:T(8,128)S(1)}, u32[]{:S(2)}, u32[]{:S(2)}) collective-permute-start(f32[36,8,256]{2,1,0:T(8,128)S(1)} %get-tuple-element.15.own_ref), channel_id=1, source_target_pairs={{8,16},{16,8},{24,32},{32,24},{40,48},{48,40},{56,64},{64,56},{72,... | collective-permute-start | bytes 884744 | tf_op jit(solution)/shard_map/ppermute | solution.py:424
  3.8 13.6 %collective-permute-start.1 = (f32[36,8,256]{2,1,0:T(8,128)S(1)}, f32[36,8,256]{2,1,0:T(8,128)S(1)}, u32[]{:S(2)}, u32[]{:S(2)}) collective-permute-start(f32[36,8,256]{2,1,0:T(8,128)S(1)} %get-tuple-element.15.own_ref), channel_id=1, source_target_pairs={{0,8},{8,0},{16,24},{24,16},{32,40},{40,32},{48,56},{56,48},{64,72... | collective-permute-start | bytes 884744 | tf_op jit(solution)/shard_map/ppermute | solution.py:425
  10.4 7.1 %collective-permute-start = (f32[18,8,256]{2,1,0:T(8,128)S(1)}, f32[18,8,256]{2,1,0:T(8,128)S(1)}, u32[]{:S(2)}, u32[]{:S(2)}) collective-permute-start(f32[18,8,256]{2,1,0:T(8,128)S(1)} %get-tuple-element.16), channel_id=1, source_target_pairs={{1,2},{2,1},{3,4},{4,3},{5,6},{6,5},{9,10},{10,9},{11,12},{12,11},... | collective-permute-start | bytes 442376 | tf_op jit(solution)/shard_map/ppermute | solution.py:426
  18.1 19.1 %collective-permute-start.4 = (f32[54,8,256]{2,1,0:T(8,128)S(1)}, f32[54,8,256]{2,1,0:T(8,128)S(1)}, u32[]{:S(2)}, u32[]{:S(2)}) collective-permute-start(f32[54,8,256]{2,1,0:T(8,128)S(1)} %get-tuple-element.18), channel_id=1, source_target_pairs={{0,1},{1,0},{2,3},{3,2},{4,5},{5,4},{6,7},{7,6},{8,9},{9,8},{10,11... | collective-permute-start | bytes 1327112 | tf_op jit(solution)/shard_map/ppermute | solution.py:438
  29.1 8.0 %collective-permute-start.3 = (f32[36,8,256]{2,1,0:T(8,128)S(1)}, f32[36,8,256]{2,1,0:T(8,128)S(1)}, u32[]{:S(2)}, u32[]{:S(2)}) collective-permute-start(f32[36,8,256]{2,1,0:T(8,128)S(1)} %get-tuple-element.17), channel_id=1, source_target_pairs={{1,2},{2,1},{3,4},{4,3},{5,6},{6,5},{9,10},{10,9},{11,12},{12,11},... | collective-permute-start | bytes 884744 | tf_op jit(solution)/shard_map/ppermute | solution.py:437
  37.1 48.2 %copy-start = (f32[60,128]{1,0:T(8,128)S(1)}, f32[60,128]{1,0:T(8,128)}, u32[]{:S(2)}) copy-start(f32[60,128]{1,0:T(8,128)} %constant.36.clone.table_ref) | copy-start | bytes 92164

commit v3 on v2

--- a/solution.py
+++ b/solution.py
@@ -91,45 +91,33 @@
     return jnp.where(low, a, pltpu.roll(b, DEPTH, 0))
 
 
-def pack_kernel(par_ref, res_hbm, diag_hbm, out_ref, next_ref, res_ref, diag_ref, sems):
-    core = par_ref[1]
-    copies = (
-        pltpu.make_async_copy(res_hbm, res_ref, sems.at[0]),
-        pltpu.make_async_copy(diag_hbm, diag_ref, sems.at[1]),
-    )
-    for copy in copies:
-        copy.start()
-    for copy in copies:
-        copy.wait()
+def pack(raw_ref, ref):
     for x in range(CX):
-        out_ref[CY * x : CY * x + CY] = jnp.swapaxes(res_ref[:, x], 0, 1)
-        out_ref[OWN + x] = diag_ref[x]
-    first = DEPTH * core
-    for x in range(CX):
-        for k in range(DEPTH):
-            next_ref[DEPTH * x + k] = out_ref[CY * x + first + k]
-    for k in range(CX // 2):
-        a, b = diag_ref[2 * k], diag_ref[2 * k + 1]
-        next_ref[CX * DEPTH + k] = jnp.where(core == 0, halves(a, b, 0), halves(a, b, DEPTH))
-
-
-def side_kernel(par_ref, own_ref, even_ref, odd_ref, next_ref, die_ref, link_ref):
-    del next_ref
-    px, core = par_ref[0], par_ref[1]
-    sides = ((own_ref, CX), (even_ref, 2 * CX * (1 - px)), (odd_ref, 2 * CX * px))
-    for which, (ref, base) in enumerate(sides):
-        packed = base // 2 if which else 0
+        ref[CY * x : CY * x + CY] = jnp.swapaxes(raw_ref[:NRHS, x], 0, 1)
+        ref[OWN + x] = raw_ref[NRHS, x]
+
+
+def rows_of(ref, base, count, up_ref, down_ref):
+    for out_ref, first in ((up_ref, CY - DEPTH), (down_ref, 0)):
         for x in range(CX):
             for k in range(DEPTH):
-                die_ref[(base + x) * DEPTH + k] = ref[CY * x + DEPTH * (1 - core) + k]
-                if which:
-                    link_ref[(packed + x) * DEPTH + k] = ref[CY * x + DEPTH * core + k]
+                out_ref[(base + x) * DEPTH + k] = ref[CY * x + first + k]
         for k in range(CX // 2):
-            a, b = ref[OWN + 2 * k], ref[OWN + 2 * k + 1]
-            low, high = halves(a, b, 0), halves(a, b, DEPTH)
-            die_ref[WX * DEPTH + base // 2 + k] = jnp.where(core == 0, high, low)
-            if which:
-                link_ref[2 * CX * DEPTH + packed // 2 + k] = jnp.where(core == 0, low, high)
+            pair = halves(ref[OWN + 2 * k], ref[OWN + 2 * k + 1], first)
+            out_ref[count * DEPTH + base // 2 + k] = pair
+
+
+def pack_kernel(raw_ref, out_ref, up_ref, down_ref):
+    pack(raw_ref, out_ref)
+    rows_of(out_ref, 0, CX, up_ref, down_ref)
+
+
+def side_kernel(evens_ref, odds_ref, up_ref, down_ref, even_ref, odd_ref):
+    px = lax.axis_index("y") & 1
+    pack(evens_ref, even_ref)
+    pack(odds_ref, odd_ref)
+    rows_of(even_ref, CX * (1 - px), 2 * CX, up_ref, down_ref)
+    rows_of(odd_ref, CX * px, 2 * CX, up_ref, down_ref)
 
 
 def place(e_ref, v_ref, level, x):
@@ -174,10 +162,11 @@
             ref[at + y] = zero
 
 
-def clear_planes(par_ref, e_ref, v_ref, level, spans):
-    for index, xs in ((2, (level, DEPTH)), (3, (DEPTH + CX, WX - level))):
-
-        @pl.when(par_ref[index] == 1)
+def clear_planes(e_ref, v_ref, level, spans):
+    at, last = lax.axis_index(GX), lax.axis_size(GX) - 1
+    for edge, xs in ((0, (level, DEPTH)), (last, (DEPTH + CX, WX - level))):
+
+        @pl.when(at == edge)
         def _(xs=xs):
             for ys in spans:
                 clear(e_ref, v_ref, level, xs, ys)
@@ -187,8 +176,8 @@
     return jnp.broadcast_to((line + (CENTRE + 1.0)) * THIRD, (NRHS, CZ))
 
 
-def inner_kernel(par_ref, own_ref, even_ref, odd_ref, e_ref, v_ref, bc_ref):
-    px = par_ref[0]
+def inner_kernel(own_ref, even_ref, odd_ref, e_ref, v_ref, bc_ref):
+    px = lax.axis_index("y") & 1
     for ref, base in ((own_ref, CX), (even_ref, 2 * CX * (1 - px)), (odd_ref, 2 * CX * px)):
         for x in range(CX):
             for y in range(CY):
@@ -198,7 +187,7 @@
     for level in range(DEPTH - 1):
         low, high = DEPTH + level + 1, DEPTH + CY - level - 1
         advance(e_ref, v_ref, bc_ref, level, range(low, high))
-        clear_planes(par_ref, e_ref, v_ref, level + 1, ((low, high),))
+        clear_planes(e_ref, v_ref, level + 1, ((low, high),))
 
 
 def split(a):
@@ -209,20 +198,24 @@
 
 
 def basis_kernel(
-    par_ref, own_ref, next_ref, link_ref, die_ref, e_in, v_in, bc_in, e_ref, v_ref, bc_ref, out_ref
+    own_ref, lows, highs, e_in, v_in, bc_in, e_ref, v_ref, bc_ref, out_ref
 ):
     del e_in, v_in, bc_in
-    core = par_ref[1]
-    die_at, link_at = 3 * DEPTH * (1 - core), 3 * DEPTH * core
-    sources = [(die_ref, x, x, WX, die_at) for x in range(WX)]
-    sources += [(next_ref, x, CX + x, CX, link_at) for x in range(CX)]
-    sources += [(link_ref, x, x if x < CX else CX + x, 2 * CX, link_at) for x in range(2 * CX)]
-    for ref, mine, x, count, base in sources:
-        for k in range(DEPTH):
-            at = x * WY + base + k
-            e_ref[0, at] = ref[mine * DEPTH + k]
-            row = DEPTH * (mine % 2) + k
-            bc_ref[at] = scaled(ref[count * DEPTH + mine // 2, row : row + 1])
+    at_y, last_y = lax.axis_index("gy"), lax.axis_size("gy") - 1
+    for (near_ref, rest_ref), base, edge in ((lows, 0, 0), (highs, DEPTH + CY, last_y)):
+        sources = [(near_ref, x, CX + x, CX) for x in range(CX)]
+        sources += [(rest_ref, x, x if x < CX else CX + x, 2 * CX) for x in range(2 * CX)]
+        for ref, mine, x, count in sources:
+            for k in range(DEPTH):
+                at = x * WY + base + k
+                e_ref[0, at] = ref[mine * DEPTH + k]
+                row = DEPTH * (mine % 2) + k
+                bc_ref[at] = scaled(ref[count * DEPTH + mine // 2, row : row + 1])
+
+        @pl.when(at_y == edge)
+        def _(base=base):
+            clear(e_ref, v_ref, 0, (0, WX), (base, base + DEPTH))
+
     for level in range(DEPTH):
         m = level + 1
         low, high = DEPTH + m, DEPTH + CY - m
@@ -233,10 +226,10 @@
         for part in rows:
             advance(e_ref, v_ref, bc_ref, level, part)
         if m < DEPTH:
-            clear_planes(par_ref, e_ref, v_ref, m, [(part[0], part[-1] + 1) for part in rows])
-            for index, ys in ((4, (m, DEPTH)), (5, (DEPTH + CY, WY - m))):
-
-                @pl.when(par_ref[index] == 1)
+            clear_planes(e_ref, v_ref, m, [(part[0], part[-1] + 1) for part in rows])
+            for edge, ys in ((0, (m, DEPTH)), (last_y, (DEPTH + CY, WY - m))):
+
+                @pl.when(at_y == edge)
                 def _(ys=ys, m=m):
                     clear(e_ref, v_ref, m, (m, WX - m), ys)
 
@@ -361,21 +354,18 @@
 
 
 VMEM = pl.BlockSpec(memory_space=pltpu.VMEM)
-SMEM = pl.BlockSpec(memory_space=pltpu.SMEM)
-HBM = pl.BlockSpec(memory_space=pltpu.HBM)
 
 
 def f32(*shape):
     return jax.ShapeDtypeStruct(shape, jnp.float32)
 
 
-def call(kernel, specs, out_shape, *args, scratch=(), limit=12, flops=10**8, aliases=None):
+def call(kernel, specs, out_shape, *args, limit=12, flops=10**8, aliases=None):
     return pl.pallas_call(
         kernel,
         in_specs=specs,
         out_specs=jax.tree.map(lambda _: VMEM, out_shape),
         out_shape=out_shape,
-        scratch_shapes=scratch,
         input_output_aliases=aliases or {},
         cost_estimate=pl.CostEstimate(flops=flops, bytes_accessed=10**6, transcendentals=0),
         compiler_params=pltpu.CompilerParams(vmem_limit_bytes=limit * 2**20),
@@ -389,6 +379,18 @@
     return out
 
 
+def exchanged(rows):
+    count = lax.axis_size("gy")
+    up = [(i, (i + 1) % count) for i in range(count)]
+    down = [(target, source) for source, target in up]
+    return lax.ppermute(rows[0], "gy", up), lax.ppermute(rows[1], "gy", down)
+
+
+def first_of(axes, at):
+    count = lax.axis_size(axes)
+    return [[(at + i) % count for i in range(count)]]
+
+
 def spread(x, axes, groups=None):
     count = lax.axis_size(axes)
     copies = jnp.broadcast_to(x[None], (count, *x.shape))
@@ -396,69 +398,33 @@
 
 
 def body(residual_block, diagonal):
-    at_x, at_y = lax.axis_index(GX), lax.axis_index("gy")
-    count_x, count_y = lax.axis_size(GX), lax.axis_size("gy")
-    par = jnp.stack(
-        [
-            at_x & 1,
-            at_y & 1,
-            at_x == 0,
-            at_x == count_x - 1,
-            at_y == 0,
-            at_y == count_y - 1,
-        ]
-    ).astype(jnp.int32)
-    own, nxt = call(
-        pack_kernel,
-        [SMEM, HBM, HBM],
-        [f32(PACK, NRHS, CZ), f32(NEXT, NRHS, CZ)],
-        par,
-        residual_block,
-        diagonal,
-        scratch=[
-            pltpu.VMEM(residual_block.shape, jnp.float32),
-            pltpu.VMEM(diagonal.shape, jnp.float32),
-            pltpu.SemaphoreType.DMA((2,)),
-        ],
-    )
-    odd = lax.ppermute(own, GX, swaps(count_x, 1))
-    even = lax.ppermute(own, GX, swaps(count_x, 0))
-    nxt = lax.ppermute(nxt, "gy", swaps(count_y, 1))
-    die, link = call(
-        side_kernel,
-        [SMEM] + [VMEM] * 4,
-        [f32(WX * DEPTH + WX // 2, NRHS, CZ), f32(REST, NRHS, CZ)],
-        par,
-        own,
-        even,
-        odd,
-        nxt,
-    )
-    link = lax.ppermute(link, "gy", swaps(count_y, 1))
-    die = lax.ppermute(die, "gy", swaps(count_y, 0))
+    count_x = lax.axis_size(GX)
+    raw = jnp.concatenate([residual_block, diagonal[None]], 0)
+    odd = lax.ppermute(raw, GX, swaps(count_x, 1))
+    even = lax.ppermute(raw, GX, swaps(count_x, 0))
+    own, *near = call(pack_kernel, [VMEM], [f32(PACK, NRHS, CZ)] + [f32(NEXT, NRHS, CZ)] * 2, raw)
+    near = exchanged(near)
+    *rest, even, odd = call(side_kernel, [VMEM] * 2, [f32(REST, NRHS, CZ)] * 2 + [f32(PACK, NRHS, CZ)] * 2, even, odd)
+    rest = exchanged(rest)
     state = [
         f32(DEPTH, WX * WY, NRHS, CZ),
         f32(DEPTH, CX * WY, NRHS, CZ),
         f32(WX * WY, NRHS, CZ),
     ]
-    e, v, bc = call(inner_kernel, [SMEM] + [VMEM] * 3, state, par, own, even, odd)
+    e, v, bc = call(inner_kernel, [VMEM] * 3, state, own, even, odd)
     e, v, bc, message = call(
         basis_kernel,
-        [SMEM] + [VMEM] * 7,
+        [VMEM, (VMEM, VMEM), (VMEM, VMEM), VMEM, VMEM, VMEM],
         [*state, f32(1, MESSAGE)],
-        par,
         own,
-        nxt,
-        link,
-        die,
+        (near[0], rest[0]),
+        (near[1], rest[1]),
         e,
         v,
         bc,
         aliases={5: 0, 6: 1, 7: 2},
     )
-    count = lax.axis_size(FAR)
-    order = [[(count // 2 + i) % count for i in range(count)]]
-    sums = spread(spread(message, NEAR).sum(0), FAR, order)
+    sums = spread(spread(message, NEAR, first_of(NEAR, 4)).sum(0), FAR, first_of(FAR, 8))
     corr, new, est = call(
         finish_kernel,
         [VMEM] * 4,

time: 88.3 us -> 83.1 us (0.941)
  blocking collectives: 44.4 us -> 46.9 us
  waiting for transfers between devices: 7.48 us -> 5.14 us
  Pallas kernels: 8.93 us -> 6.63 us
  starting transfers between devices: 24.4 us -> 22.3 us
  local copies, waits for them, and re-layouts: 1.87 us -> 0.08 us
  other arithmetic: 0.12 us -> 1.11 us
    all_to_all x2, blocking collectives: 44.4 us -> 46.9 us  [spread(): lax.all_to_all(copies, axes, 0, 0, tiled=True, axis_index_groups=groups)]
    ppermute x5 -> x6, waiting for transfers between devices: 7.48 us -> 5.14 us  [the longest x1 4.09 us: body(): even = lax.ppermute(raw, GX, swaps(count_x, 0))]
    pallas_call x5, Pallas kernels: 8.93 us -> 6.63 us  [call(): pl.pallas_call(kernel, in_specs=specs, out_specs=jax.tree.map(lambda _: V...]
    ppermute x5 -> x6, starting transfers between devices: 24.4 us -> 22.3 us  [the longest x4 15.1 us: exchanged(): return (lax.ppermute(rows[0], 'gy', up), lax.ppermute(rows[1], 'gy', down))]
    unnamed x6 -> x2, local copies, waits for them, and re-layouts: 1.71 us -> 0.01 us
    concatenate x0 -> x1, other arithmetic: none -> 0.99 us  [body(): raw = jnp.concatenate([residual_block, diagonal[None]], 0)]
  transfers between devices with their start and end apart: 5 -> 6, of which waited for: 2 -> 2; matrix products, arithmetic and copies ran while one was open for 0% -> 0% of each run, Pallas kernels for 2% -> 1%
where the time goes in v3:
time: 83.1 us; the launch traced here: 82.9 us
  blocking collectives  46.9 us (56%)
  starting transfers between devices  22.3 us (27%)
  Pallas kernels  6.63 us (8%)
  waiting for transfers between devices  5.14 us (6%)
  other arithmetic  1.11 us (1%)
    all_to_all x2, blocking collectives, spread(): lax.all_to_all(copies, axes, 0, 0, tiled=True, axis_index_groups=groups)  46.9 us
    ppermute x4, starting transfers between devices, exchanged(): return (lax.ppermute(rows[0], 'gy', up), lax.ppermute(rows[1], 'gy', down))  15.1 us
    pallas_call x5, Pallas kernels, call(): pl.pallas_call(kernel, in_specs=specs, out_specs=jax.tree.map(lambda _: V...  6.63 us
    ppermute x1, starting transfers between devices, body(): even = lax.ppermute(raw, GX, swaps(count_x, 0))  6.55 us
    ppermute x1, waiting for transfers between devices, body(): even = lax.ppermute(raw, GX, swaps(count_x, 0))  4.09 us
  transfers between devices with their start and end apart: 6, of which 2 were waited for; matrix products, arithmetic and copies ran while one was open for 0% of the time, Pallas kernels for 1%

profile of v3, /device:TPU:1, one launch (start us, length us, event | category | flops | bytes accessed | tf_op | source)
XLA Modules:
  0.0 82.9 jit_solution(9729820996990141596)
XLA Ops:
  0.6 1.0 %pad_maximum_fusion.raw_ref = f32[9,4,8,256]{3,2,1,0:T(8,128)S(1)} fusion(f32[1,4,8,256]{3,2,1,0:T(8,128)} %bitcast.2, f32[8,4,8,256]{3,2,1,0:T(8,128)} %param.3), kind=kLoop, calls=%fused_computation | loop fusion | flops 73728 | bytes 589824 | tf_op jit(solution)/shard_map/concatenate | solution.py:402
  1.6 0.7 collective-permute-start.2
  2.3 6.5 %collective-permute-start.1 = (f32[9,4,8,256]{3,2,1,0:T(8,128)S(1)}, f32[9,4,8,256]{3,2,1,0:T(8,128)S(1)}, u32[]{:S(2)}, u32[]{:S(2)}) collective-permute-start(f32[9,4,8,256]{3,2,1,0:T(8,128)S(1)} %pad_maximum_fusion.raw_ref), channel_id=1, source_target_pairs={{0,8},{8,0},{16,24},{24,16},{32,40},{40,32},{48,56},{56,48},{64,72... | collective-permute-start | bytes 884744 | tf_op jit(solution)/shard_map/ppermute | solution.py:404
  8.9 0.0 collective-permute-done.2.odds_ref
  8.9 4.1 %collective-permute-done.1.evens_ref = f32[9,4,8,256]{3,2,1,0:T(8,128)S(1)} collective-permute-done((f32[9,4,8,256]{3,2,1,0:T(8,128)S(1)}, f32[9,4,8,256]{3,2,1,0:T(8,128)S(1)}, u32[]{:S(2)}, u32[]{:S(2)}) %collective-permute-start.1) | collective-permute-done | bytes 294944 | tf_op jit(solution)/shard_map/ppermute | solution.py:404
  13.0 0.1 shard_map.59
  13.1 5.0 %collective-permute-start.3 = (f32[36,8,256]{2,1,0:T(8,128)S(1)}, f32[36,8,256]{2,1,0:T(8,128)S(1)}, u32[]{:S(2)}, u32[]{:S(2)}) collective-permute-start(f32[36,8,256]{2,1,0:T(8,128)S(1)} %get-tuple-element.20), channel_id=1, source_target_pairs={{0,1},{1,2},{2,3},{3,4},{4,5},{5,6},{6,7},{7,0},{8,9},{9,10},{10,1... | collective-permute-start | bytes 884744 | tf_op jit(solution)/shard_map/ppermute | solution.py:386
  18.1 7.2 %collective-permute-start.5 = (f32[36,8,256]{2,1,0:T(8,128)S(1)}, f32[36,8,256]{2,1,0:T(8,128)S(1)}, u32[]{:S(2)}, u32[]{:S(2)}) collective-permute-start(f32[36,8,256]{2,1,0:T(8,128)S(1)} %get-tuple-element.22), channel_id=1, source_target_pairs={{1,0},{2,1},{3,2},{4,3},{5,4},{6,5},{7,6},{0,7},{9,8},{10,9},{11,1... | collective-permute-start | bytes 884744 | tf_op jit(solution)/shard_map/ppermute | solution.py:386
  25.2 0.1 shard_map.58
  25.3 0.0 collective-permute-start
  25.3 2.9 %collective-permute-start.4 = (f32[18,8,256]{2,1,0:T(8,128)S(1)}, f32[18,8,256]{2,1,0:T(8,128)S(1)}, u32[]{:S(2)}, u32[]{:S(2)}) collective-permute-start(f32[18,8,256]{2,1,0:T(8,128)S(1)} %get-tuple-element.21), channel_id=1, source_target_pairs={{1,0},{2,1},{3,2},{4,3},{5,4},{6,5},{7,6},{0,7},{9,8},{10,9},{11,1... | collective-permute-start | bytes 442376 | tf_op jit(solution)/shard_map/ppermute | solution.py:386
  28.2 0.9 %shard_map.60 = (f32[4,192,8,256]{3,2,1,0:T(8,128)S(1)}, f32[4,64,8,256]{3,2,1,0:T(8,128)S(1)}, f32[192,8,256]{2,1,0:T(8,128)S(1)}) custom-call(f32[36,8,256]{2,1,0:T(8,128)S(1)} %get-tuple-element.18.own_ref, f32[36,8,256]{2,1,0:T(8,128)S(1)} %get-tuple-element.23.even_ref, f32[36,8,256]{2,1,0:T(8,128)S(1)} %get-tuple-element.24.odd_ref), custom_call_target="tpu_custom_call" | custom-call | flops 100000000 | bytes 1000000 | tf_op jit(solution)/shard_map/pallas_call | solution.py:364
  29.1 0.0 collective-permute-done.lows_0_
  29.1 1.0 %collective-permute-done.4.highs_0_ = f32[18,8,256]{2,1,0:T(8,128)S(1)} collective-permute-done((f32[18,8,256]{2,1,0:T(8,128)S(1)}, f32[18,8,256]{2,1,0:T(8,128)S(1)}, u32[]{:S(2)}, u32[]{:S(2)}) %collective-permute-start.4) | collective-permute-done | bytes 147488 | tf_op jit(solution)/shard_map/ppermute | solution.py:386
  30.2 0.0 collective-permute-done.3.lows_1_
  30.2 0.0 collective-permute-done.5.highs_1_
  30.2 0.0 copy-start
  30.2 3.0 %shard_map.61 = (f32[4,192,8,256]{3,2,1,0:T(8,128)S(1)}, f32[4,64,8,256]{3,2,1,0:T(8,128)S(1)}, f32[192,8,256]{2,1,0:T(8,128)S(1)}, f32[1,384]{1,0:T(1,128)S(1)}) custom-call(f32[36,8,256]{2,1,0:T(8,128)S(1)} %get-tuple-element.18.own_ref, ...), custom_call_target="tpu_custom_call", output_to_operand_aliasing={{0}: (5, {}), {1}: (6, {}), {2}: (7, {})} | custom-call | flops 100000000 | bytes 1000000 | tf_op jit(solution)/shard_map/pallas_call | solution.py:364
  33.2 0.1 broadcast_in_dim.19
  33.2 15.5 %all_to_all.10 = f32[64,1,384]{2,1,0:T(1,128)S(1)} all-to-all(f32[64,1,384]{2,1,0:T(1,128)S(1)} %broadcast_in_dim.19), channel_id=1, replica_groups={{4,5,6,7,8,9,10,11,12,13,14,15,16,17,18,19,20,21,22,23,24,25,26,27,28,2..., dimensions={0} | all-to-all | bytes 196608 | tf_op jit(solution)/shard_map/all_to_all | solution.py:397
  48.7 0.1 reduce_sum.9
  48.8 31.4 %all_to_all.11.sums_ref = f32[16,1,384]{2,1,0:T(1,128)S(1)} all-to-all(f32[16,1,384]{2,1,0:T(1,128)S(1)} %broadcast_in_dim.20), channel_id=1, replica_groups={{512,576,640,704,768,832,896,960,0,64,128,192,256,320,384,448},{513,577..., dimensions={0} | all-to-all | bytes 49152 | tf_op jit(solution)/shard_map/all_to_all | solution.py:397
  80.2 0.0 copy-done
  80.2 2.6 %shard_map.62 = (f32[8,4,8,256]{3,2,1,0:T(8,128)}, f32[8,4,8,256]{3,2,1,0:T(8,128)}, f32[1,8]{1,0:T(1,128)}) custom-call(f32[60,128]{1,0:T(8,128)S(1)} %copy-done, f32[16,1,384]{2,1,0:T(1,128)S(1)} %all_to_all.11.sums_ref, f32[36,8,256]{2,1,0:T(8,128)S(1)} %get-tuple-element.18.own_ref, f32[4,64,8,256]{3,2,1,0:T(8,128)S(1)} %get-tuple-element.29.v_ref), custom_call_target="tpu_custom_call" | custom-call | flops 100000000 | bytes 1000000 | tf_op jit(solution)/shard_map/pallas_call | solution.py:364
  (2 shorter events, 0.0 us)
Async XLA Ops:
  1.6 7.2 %collective-permute-start.2 = (f32[9,4,8,256]{3,2,1,0:T(8,128)S(1)}, f32[9,4,8,256]{3,2,1,0:T(8,128)S(1)}, u32[]{:S(2)}, u32[]{:S(2)}) collective-permute-start(f32[9,4,8,256]{3,2,1,0:T(8,128)S(1)} %pad_maximum_fusion.raw_ref), channel_id=1, source_target_pairs={{8,16},{16,8},{24,32},{32,24},{40,48},{48,40},{56,64},{64,56},{72,... | collective-permute-start | bytes 884744 | tf_op jit(solution)/shard_map/ppermute | solution.py:403
  2.3 10.7 %collective-permute-start.1 = (f32[9,4,8,256]{3,2,1,0:T(8,128)S(1)}, f32[9,4,8,256]{3,2,1,0:T(8,128)S(1)}, u32[]{:S(2)}, u32[]{:S(2)}) collective-permute-start(f32[9,4,8,256]{3,2,1,0:T(8,128)S(1)} %pad_maximum_fusion.raw_ref), channel_id=1, source_target_pairs={{0,8},{8,0},{16,24},{24,16},{32,40},{40,32},{48,56},{56,48},{64,72... | collective-permute-start | bytes 884744 | tf_op jit(solution)/shard_map/ppermute | solution.py:404
  13.1 17.1 %collective-permute-start.3 = (f32[36,8,256]{2,1,0:T(8,128)S(1)}, f32[36,8,256]{2,1,0:T(8,128)S(1)}, u32[]{:S(2)}, u32[]{:S(2)}) collective-permute-start(f32[36,8,256]{2,1,0:T(8,128)S(1)} %get-tuple-element.20), channel_id=1, source_target_pairs={{0,1},{1,2},{2,3},{3,4},{4,5},{5,6},{6,7},{7,0},{8,9},{9,10},{10,1... | collective-permute-start | bytes 884744 | tf_op jit(solution)/shard_map/ppermute | solution.py:386
  18.1 12.1 %collective-permute-start.5 = (f32[36,8,256]{2,1,0:T(8,128)S(1)}, f32[36,8,256]{2,1,0:T(8,128)S(1)}, u32[]{:S(2)}, u32[]{:S(2)}) collective-permute-start(f32[36,8,256]{2,1,0:T(8,128)S(1)} %get-tuple-element.22), channel_id=1, source_target_pairs={{1,0},{2,1},{3,2},{4,3},{5,4},{6,5},{7,6},{0,7},{9,8},{10,9},{11,1... | collective-permute-start | bytes 884744 | tf_op jit(solution)/shard_map/ppermute | solution.py:386
  25.3 3.8 %collective-permute-start = (f32[18,8,256]{2,1,0:T(8,128)S(1)}, f32[18,8,256]{2,1,0:T(8,128)S(1)}, u32[]{:S(2)}, u32[]{:S(2)}) collective-permute-start(f32[18,8,256]{2,1,0:T(8,128)S(1)} %get-tuple-element.19), channel_id=1, source_target_pairs={{0,1},{1,2},{2,3},{3,4},{4,5},{5,6},{6,7},{7,0},{8,9},{9,10},{10,1... | collective-permute-start | bytes 442376 | tf_op jit(solution)/shard_map/ppermute | solution.py:386
  25.3 4.9 %collective-permute-start.4 = (f32[18,8,256]{2,1,0:T(8,128)S(1)}, f32[18,8,256]{2,1,0:T(8,128)S(1)}, u32[]{:S(2)}, u32[]{:S(2)}) collective-permute-start(f32[18,8,256]{2,1,0:T(8,128)S(1)} %get-tuple-element.21), channel_id=1, source_target_pairs={{1,0},{2,1},{3,2},{4,3},{5,4},{6,5},{7,6},{0,7},{9,8},{10,9},{11,1... | collective-permute-start | bytes 442376 | tf_op jit(solution)/shard_map/ppermute | solution.py:386
  30.2 50.1 %copy-start = (f32[60,128]{1,0:T(8,128)S(1)}, f32[60,128]{1,0:T(8,128)}, u32[]{:S(2)}) copy-start(f32[60,128]{1,0:T(8,128)} %constant.4.clone.table_ref) | copy-start | bytes 92164
